TPU v7x, 32 devices: a whole 2x2x4 slice. The times are simulated.
32 devices in a mesh: ta: 4 (over y, x), gz: 2 (over core), xy: 4 (over z).
Axes of the slice: x: 2, y: 2, z: 4, core: 2. Of those that a mesh axis runs over, the one named last changes fastest.
Arguments:
- source: float32 [2, 4, 3, 16, 16, 512], P(None, None, None, 'ta', 'gz', 'xy'), may hold values from -6 to 6
- iterate: float32 [2, 4, 3, 16, 16, 512], P(None, None, None, 'ta', 'gz', 'xy'), may hold values from -6 to 6
- gauge_links: float32 [4, 2, 3, 3, 16, 16, 512], P(None, None, None, None, 'ta', 'gz', 'xy'), may hold values from -2.4 to 2.4
- clover: float32 [2, 2, 6, 6, 16, 16, 512], P(None, None, None, None, 'ta', 'gz', 'xy'), may hold values from -0.6 to 0.6
- bc_sign: int32 [4], replicated, may hold values from -1 to 1, as said below
- null_store: bfloat16 [4, 4, 4, 2, 24, 12, 4, 4, 128], P('ta', 'gz', 'xy'), may hold values from -0.109375 to 0.109375
- block_slot: int32 [4, 4, 4], P('ta', 'gz', 'xy'), may hold values from 0 to 1, as said below
- coarse_links: float32 [9, 2, 24, 24, 4, 4, 4, 8], P(None, None, None, None, 'ta', 'gz', 'xy'), may hold values from -0.2 to 0.2
Outputs:
- new_iterate: float32 [2, 4, 3, 16, 16, 512], P(None, None, None, 'ta', 'gz', 'xy')
- new_residual: float32 [2, 4, 3, 16, 16, 512], P(None, None, None, 'ta', 'gz', 'xy')
Inputs may be any that keep to these rules, and one draw needn't show every extreme that they name: `bc_sign`: each entry is -1 or +1. `block_slot`: within each device's block of 2 aggregate columns the entries are the numbers 0 to 1, each once.
All inputs are finite; a program needn't handle non-finite values.
Results may differ from a plain program's by a relative error of at most 0.0016.
Values sent between devices are 32-bit elements; how exact they have to be, the bound alone decides.
A program may use at most 256 MiB of HBM per device.

v0:
```python
import functools

import jax
import jax.numpy as jnp
from jax import lax
from jax.experimental import pallas as pl
from jax.experimental.pallas import tpu as pltpu
from jax.sharding import PartitionSpec as P

BLK = 4
LY = 32
CITERS = 4
MASS_TERM = 3.8
RELAX_WEIGHT = 0.4
HIGHEST = lax.Precision.HIGHEST
MESH = pl.DeviceIdType.MESH
LANES = 32
F32 = jnp.float32

UPPER = [((0, 0), (1, 0)), ((0, 3), (1, 1)), ((1, 3), (0, 3)), ((1, 2), (0, 0))]
LOWER = [((0, 0), (1, 0)), ((0, 1), (1, 3)), ((1, 1), (0, 1)), ((1, 0), (0, 2))]


def add_turned(a, b, power):
    power %= 4
    if power == 0:
        return (a[0] + b[0], a[1] + b[1])
    if power == 1:
        return (a[0] - b[1], a[1] + b[0])
    if power == 2:
        return (a[0] - b[0], a[1] - b[1])
    return (a[0] + b[1], a[1] - b[0])


def project(psi, mu, forward):
    turn = 2 if forward else 0
    return [
        [add_turned(psi[row][c], psi[2 + UPPER[mu][row][0]][c], UPPER[mu][row][1] + turn) for c in range(3)]
        for row in range(2)
    ]


def rebuild(total, half, mu, forward):
    turn = 2 if forward else 0
    for row in range(2):
        index, power = LOWER[mu][row]
        for c in range(3):
            total[row][c] = add_turned(total[row][c], half[row][c], 0)
            total[2 + row][c] = add_turned(total[2 + row][c], half[index][c], power + turn)


def link_times(gauge, mu, t, half):
    out = [[None] * 3 for _ in range(2)]
    for a in range(3):
        for b in range(3):
            ur = gauge[mu, 0, a * 3 + b, t]
            ui = gauge[mu, 1, a * 3 + b, t]
            for s in range(2):
                hr, hi = half[s][b]
                term = (ur * hr - ui * hi, ur * hi + ui * hr)
                out[s][a] = term if b == 0 else add_turned(out[s][a], term, 0)
    return out


def link_dagger(gauge, mu, t, half):
    out = [[None] * 3 for _ in range(2)]
    for a in range(3):
        for b in range(3):
            ur = gauge[mu, 0, b * 3 + a, t]
            ui = gauge[mu, 1, b * 3 + a, t]
            for s in range(2):
                hr, hi = half[s][b]
                term = (ur * hr + ui * hi, ur * hi - ui * hr)
                out[s][a] = term if b == 0 else add_turned(out[s][a], term, 0)
    return out


def load_spinor(ref, t):
    return [[(ref[s * 3 + c, t], ref[12 + s * 3 + c, t]) for c in range(3)] for s in range(4)]


def load_half(ref, *lead):
    return [[(ref[(*lead, s * 3 + c)], ref[(*lead, 6 + s * 3 + c)]) for c in range(3)] for s in range(2)]


def store_half(ref, half, *lead):
    for s in range(2):
        for c in range(3):
            ref[(*lead, s * 3 + c)] = half[s][c][0]
            ref[(*lead, 6 + s * 3 + c)] = half[s][c][1]


def map_half(half, change):
    return [[(change(z[0]), change(z[1])) for z in row] for row in half]


def roll(value, shift, axis):
    shift %= value.shape[axis]
    return value if shift == 0 else pltpu.roll(value, shift, axis)


def split_columns(a, b, top):
    return (
        jnp.where(top, a, pltpu.roll(b, BLK, 0)),
        jnp.where(top, pltpu.roll(a, BLK, 0), b),
    )


def kernel(
    counts, bc_ref, slot_ref, src_hbm, it_hbm, ga_hbm, cl_hbm, nu_hbm, co_hbm, out_it, out_res,
    src, itv, ga, cl, nu, co, res, corr, nit, ht, gt, hb, hs, ps, pr, rc, mrows, wbuf, rhs, wr, part, wexp,
    load_sem, send_sem, recv_sem,
):
    T = itv.shape[1]
    loads = []
    for i, (a, b) in enumerate(
        [(it_hbm, itv), (ga_hbm, ga), (src_hbm, src), (cl_hbm, cl), (nu_hbm, nu), (co_hbm, co)]
    ):
        copy = pltpu.make_async_copy(a, b, load_sem.at[i])
        copy.start()
        loads.append(copy)

    names = ("ta", "gz", "xy")
    place = {n: lax.axis_index(n) for n in names}
    ahead = {n: {n: lax.rem(place[n] + 1, counts[n])} for n in names}
    behind = {n: {n: lax.rem(place[n] + counts[n] - 1, counts[n])} for n in names}
    barrier = pltpu.get_barrier_semaphore()
    for n in names:
        for target in (ahead[n], behind[n]):
            pl.semaphore_signal(barrier, inc=1, device_id=target, device_id_type=MESH)

    def send(number, source, target, device):
        copy = pltpu.make_async_remote_copy(
            src_ref=source, dst_ref=target, send_sem=send_sem.at[number], recv_sem=recv_sem.at[number],
            device_id=device, device_id_type=MESH,
        )
        copy.start()
        return copy

    row = lax.broadcasted_iota(jnp.int32, (8, 128), 0)
    lane = lax.broadcasted_iota(jnp.int32, (8, 128), 1)
    column_y = lane & (LY - 1)
    sign = [bc_ref[mu].astype(F32) for mu in range(4)]
    last = [jnp.where(place[n] == counts[n] - 1, sign[i], 1.0) for i, n in enumerate(names)]
    first = [jnp.where(place[n] == 0, sign[i], 1.0) for i, n in enumerate(names)]

    def subtract_fine(d, field, base, out, before_local):
        def prepare(t, carry):
            psi = load_spinor(field, t)
            store_half(ht, project(psi, 0, True), d, t)
            store_half(gt, link_dagger(ga, 0, t, project(psi, 0, False)), d, t + 1)
            for mu in (1, 2):
                store_half(hb, project(psi, mu, True), 2 * mu - 2, t)
                store_half(hb, link_dagger(ga, mu, t, project(psi, mu, False)), 2 * mu - 1, t)
            return carry

        lax.fori_loop(0, T, prepare, 0)

        def pack(g, carry):
            for k in range(4):
                c = g * 4 + k
                z0, z1, x0, x1 = hb[0, 0, c], roll(hb[1, 0, c], 1, 0), hb[2, 0, c], roll(hb[3, 0, c], LY, 1)
                for t in range(1, T):
                    z0 = jnp.where(row == t, roll(hb[0, t, c], t, 0), z0)
                    z1 = jnp.where(row == t, roll(hb[1, t, c], t + 1, 0), z1)
                    mine = (lane // LY) == t
                    x0 = jnp.where(mine, roll(hb[2, t, c], LY * t, 1), x0)
                    x1 = jnp.where(mine, roll(hb[3, t, c], LY * t + LY, 1), x1)
                for kind, value in enumerate((z0, z1, x0, x1)):
                    ps[d, kind, c] = value
            return carry

        if d == 0:
            pl.semaphore_wait(barrier, 6)
        base_number = d * 6
        copies = [
            send(base_number, ht.at[d, 0], ht.at[d, T], behind["ta"]),
            send(base_number + 1, gt.at[d, T], gt.at[d, 0], ahead["ta"]),
        ]
        lax.fori_loop(0, 3, pack, 0)
        targets = (behind["gz"], ahead["gz"], behind["xy"], ahead["xy"])
        for kind, target in sorted(enumerate(targets), key=lambda entry: -entry[0]):
            copies.append(send(base_number + 2 + kind, ps.at[d, kind], pr.at[d, kind], target))

        before_local()

        def local(t, carry):
            psi = load_spinor(field, t)
            total = [[(jnp.zeros((8, 128), F32), jnp.zeros((8, 128), F32)) for _ in range(3)] for _ in range(4)]

            def up(v):
                return jnp.where(column_y == LY - 1, roll(v, LY - 1, 1) * sign[3], roll(v, -1, 1))

            def down(v):
                return jnp.where(column_y == 0, roll(v, 1 - LY, 1) * sign[3], roll(v, 1, 1))

            rebuild(total, link_times(ga, 3, t, map_half(project(psi, 3, True), up)), 3, True)
            rebuild(total, map_half(link_dagger(ga, 3, t, project(psi, 3, False)), down), 3, False)
            for ch in range(2):
                for i in range(6):
                    s, c = 2 * ch + i // 3, i % 3
                    re, im = psi[s][c][0] * MASS_TERM, psi[s][c][1] * MASS_TERM
                    for j in range(6):
                        vr, vi = psi[2 * ch + j // 3][j % 3]
                        mr, mi = cl[ch, 0, i * 6 + j, t], cl[ch, 1, i * 6 + j, t]
                        re = re + (mr * vr - mi * vi)
                        im = im + (mr * vi + mi * vr)
                    k = s * 3 + c
                    out[k, t] = base[k, t] - re + 0.5 * total[s][c][0]
                    out[12 + k, t] = base[12 + k, t] - im + 0.5 * total[s][c][1]
            return carry

        lax.fori_loop(0, T, local, 0)
        for copy in copies:
            copy.wait()

        def unpack(g, carry):
            for k in range(4):
                c = g * 4 + k
                z0, z1 = pr[d, 0, c] * last[1], pr[d, 1, c] * first[1]
                x0, x1 = pr[d, 2, c] * last[2], pr[d, 3, c] * first[2]
                new = []
                for t in range(T):
                    new.append((
                        jnp.where(row == 7, roll(z0, 7 - t, 0), roll(hb[0, t, c], -1, 0)),
                        jnp.where(row == 0, roll(z1, -t, 0), roll(hb[1, t, c], 1, 0)),
                        jnp.where(lane >= 128 - LY, roll(x0, 128 - LY - LY * t, 1), roll(hb[2, t, c], -LY, 1)),
                        jnp.where(lane < LY, roll(x1, -LY * t, 1), roll(hb[3, t, c], LY, 1)),
                    ))
                for t in range(T):
                    for kind in range(4):
                        hs[kind, t, c] = new[t][kind]
            return carry

        lax.fori_loop(0, 3, unpack, 0)

        def finish(t, carry):
            total = [[(jnp.zeros((8, 128), F32), jnp.zeros((8, 128), F32)) for _ in range(3)] for _ in range(4)]
            edge = jnp.where(t == T - 1, last[0], 1.0)
            rebuild(total, link_times(ga, 0, t, map_half(load_half(ht, d, t + 1), lambda v: v * edge)), 0, True)
            low = jnp.where(t == 0, first[0], 1.0)
            rebuild(total, map_half(load_half(gt, d, t), lambda v: v * low), 0, False)
            for mu in (1, 2):
                rebuild(total, link_times(ga, mu, t, load_half(hs, 2 * mu - 2, t)), mu, True)
                rebuild(total, load_half(hs, 2 * mu - 1, t), mu, False)
            for s in range(4):
                for c in range(3):
                    k = s * 3 + c
                    out[k, t] = out[k, t] + 0.5 * total[s][c][0]
                    out[12 + k, t] = out[12 + k, t] + 0.5 * total[s][c][1]
            return carry

        lax.fori_loop(0, T, finish, 0)

    mrows[...] = jnp.zeros(mrows.shape, F32)
    loads[0].wait()
    loads[1].wait()

    def rest():
        loads[2].wait()
        loads[3].wait()

    subtract_fine(0, itv, src, res, rest)

    top = row < BLK

    def to_columns(k, carry):
        for pair in range(2):
            parts = split_columns(res[k, 2 * pair], res[k, 2 * pair + 1], top)
            for col in range(2):
                rc[col, k, pl.ds(8 * pair, 8), :] = parts[col].astype(jnp.bfloat16).astype(F32)
        return carry

    lax.fori_loop(0, 24, to_columns, 0)
    loads[4].wait()
    group = 4
    for col in range(2):
        slot = slot_ref[col]

        def restrict(g, carry):
            re = [jnp.zeros((16, 128), F32) for _ in range(group)]
            im = [jnp.zeros((16, 128), F32) for _ in range(group)]
            for s in range(12):
                fr, fi = rc[col, s], rc[col, 12 + s]
                for j in range(group):
                    nr = nu[slot, 0, g * group + j, s].astype(F32)
                    ni = nu[slot, 1, g * group + j, s].astype(F32)
                    re[j] = re[j] + (nr * fr + ni * fi)
                    im[j] = im[j] + (nr * fi - ni * fr)
            for j in range(group):
                mrows[pl.ds((2 * col) * LANES + g * group + j, 1), :] = jnp.sum(re[j], axis=0, keepdims=True)
                mrows[pl.ds((2 * col + 1) * LANES + g * group + j, 1), :] = jnp.sum(im[j], axis=0, keepdims=True)
            return carry

        lax.fori_loop(0, 24 // group, restrict, 0)
    chooser = ((column_y // BLK) == row).astype(F32)
    value = lax.dot_general(
        chooser, mrows[...], (((1,), (1,)), ((), ())), precision=HIGHEST, preferred_element_type=F32
    )
    rhs[...] = value
    wbuf[0] = RELAX_WEIGHT * value
    loads[5].wait()

    nv = co.shape[-1]
    block = 8
    def pieces(vector, col):
        return [roll(vector, -LANES * (2 * col + ri), 1)[:, :nv] for ri in range(2)]

    def products(col, pairs, i, re, im):
        for k, (vr, vi) in pairs:
            yr, yi = co[k, 0, i, col], co[k, 1, i, col]
            a, b = yr * vr - yi * vi, yr * vi + yi * vr
            re, im = (a, b) if re is None else (re + a, im + b)
        return re, im

    for it in range(CITERS - 1):
        targets = [ahead["ta"], behind["ta"], ahead["gz"], behind["gz"], ahead["xy"], behind["xy"]]
        copies = [None] * 6
        for d in (4, 5, 0, 1, 2, 3):
            copies[d] = send(12 + it * 6 + d, wbuf.at[it], wr.at[it, d], targets[d ^ 1])
        own = wbuf[it]
        up, down = roll(own, -1, 0), roll(own, 1, 0)
        copies[2].wait()
        copies[3].wait()
        next_z, last_z = wr[it, 2], wr[it, 3]
        pairs = [
            [
                (0, pieces(own, col)),
                (7, pieces(up, col)),
                (8, pieces(down, col)),
                (3, pieces(own, 1) if col == 0 else pieces(next_z, 0)),
                (4, pieces(own, 0) if col == 1 else pieces(last_z, 1)),
            ]
            for col in range(2)
        ]

        def near(g, carry):
            for j in range(block):
                i = g * block + j
                for col in range(2):
                    re, im = products(col, pairs[col], i, None, None)
                    part[col, 0, i] = re
                    part[col, 1, i] = im
            return carry

        lax.fori_loop(0, nv // block, near, 0)
        for d in (0, 1, 4, 5):
            copies[d].wait()
        far_pairs = [
            [(k, pieces(wr[it, d], col)) for k, d in ((1, 0), (2, 1), (5, 4), (6, 5))] for col in range(2)
        ]

        def far(g, applied):
            for j in range(block):
                i = g * block + j
                for col in range(2):
                    sums = products(col, far_pairs[col], i, part[col, 0, i], part[col, 1, i])
                    for ri in range(2):
                        whole = jnp.sum(sums[ri], axis=1, keepdims=True)
                        applied = jnp.where(lane == LANES * (2 * col + ri) + i, whole, applied)
            return applied

        applied = lax.fori_loop(0, nv // block, far, jnp.zeros((8, 128), F32))
        w = wbuf[it]
        wbuf[it + 1] = w + RELAX_WEIGHT * (rhs[...] - (2.0 * w + applied))

    w = wbuf[CITERS - 1].astype(jnp.bfloat16).astype(F32)
    wexp[...] = lax.dot_general(
        w, chooser, (((0,), (0,)), ((), ())), precision=HIGHEST, preferred_element_type=F32
    )
    spins = 3
    step = 4
    for col in range(2):
        slot = slot_ref[col]

        def some_spins(q, carry):
            def over(g, totals):
                totals = list(totals)
                for j in range(step):
                    c = g * step + j
                    vr = wexp[pl.ds(2 * col * LANES + c, 1), :]
                    vi = wexp[pl.ds((2 * col + 1) * LANES + c, 1), :]
                    for m in range(spins):
                        nr = nu[slot, 0, c, q * spins + m].astype(F32)
                        ni = nu[slot, 1, c, q * spins + m].astype(F32)
                        totals[2 * m] = totals[2 * m] + (nr * vr - ni * vi)
                        totals[2 * m + 1] = totals[2 * m + 1] + (nr * vi + ni * vr)
                return tuple(totals)

            zero = jnp.zeros((16, 128), F32)
            totals = lax.fori_loop(0, nv // step, over, (zero,) * (2 * spins))
            for m in range(spins):
                rc[col, q * spins + m] = totals[2 * m]
                rc[col, 12 + q * spins + m] = totals[2 * m + 1]
            return carry

        lax.fori_loop(0, 12 // spins, some_spins, 0)

    def from_columns(k, carry):
        for pair in range(2):
            part_0 = rc[0, k, pl.ds(8 * pair, 8), :]
            part_1 = rc[1, k, pl.ds(8 * pair, 8), :]
            values = split_columns(part_0, part_1, top)
            for h in range(2):
                t = 2 * pair + h
                corr[k, t] = values[h]
                nit[k, t] = itv[k, t] + values[h]
        return carry

    lax.fori_loop(0, 24, from_columns, 0)
    store_it = pltpu.make_async_copy(nit, out_it, load_sem.at[6])
    store_it.start()
    subtract_fine(1, corr, res, res, lambda: None)
    store_res = pltpu.make_async_copy(res, out_res, load_sem.at[7])
    store_res.start()
    store_it.wait()
    store_res.wait()


def hand_over(it_in, res_in, it_out, res_out, it_mid, res_mid, sem):
    ways = [(it_in, it_mid, it_out), (res_in, res_mid, res_out)]
    inward = [pltpu.make_async_copy(a, b, sem.at[i]) for i, (a, b, _) in enumerate(ways)]
    outward = [pltpu.make_async_copy(b, c, sem.at[2 + i]) for i, (_, b, c) in enumerate(ways)]
    for copy in inward:
        copy.start()
    for first, second in zip(inward, outward):
        first.wait()
        second.start()
    for copy in outward:
        copy.wait()


def per_device(counts, source, iterate, gauge_links, clover, bc_sign, null_store, block_slot, coarse_links):
    lattice = source.shape[3:]
    T = lattice[0]
    spinor = (24,) + lattice
    columns = block_slot.size
    nv = null_store.shape[4]
    assert lattice == (BLK, 2 * BLK, BLK * LY) and columns == 2
    nulls = (columns,) + null_store.shape[3:6] + (BLK * BLK, BLK * LY)
    links = jnp.transpose(coarse_links, (0, 1, 2, 4, 5, 6, 7, 3))
    links = links.reshape(links.shape[:3] + (columns,) + links.shape[6:])
    gauge_shape = (4, 2, 9) + lattice
    clover_shape = (2, 2, 36) + lattice
    half = (12,) + lattice[1:]
    tile = lattice[1:]
    smem = pl.BlockSpec(memory_space=pltpu.SMEM)
    hbm = pl.BlockSpec(memory_space=pl.ANY)
    fine = jax.ShapeDtypeStruct(spinor, F32)
    n_copies = 12 + 6 * (CITERS - 1)
    outs = pl.pallas_call(
        functools.partial(kernel, counts),
        out_shape=(fine, fine),
        in_specs=[smem, smem] + [pl.BlockSpec(memory_space=pltpu.HBM)] * 6,
        out_specs=(hbm, hbm),
        scratch_shapes=[
            pltpu.VMEM(spinor, F32),
            pltpu.VMEM(spinor, F32),
            pltpu.VMEM(gauge_shape, F32),
            pltpu.VMEM(clover_shape, F32),
            pltpu.VMEM(nulls, jnp.bfloat16),
            pltpu.VMEM(links.shape, F32),
            pltpu.VMEM(spinor, F32),
            pltpu.VMEM(spinor, F32),
            pltpu.VMEM(spinor, F32),
            pltpu.VMEM((2, T + 1) + half, F32),
            pltpu.VMEM((2, T + 1) + half, F32),
            pltpu.VMEM((4, T) + half, F32),
            pltpu.VMEM((4, T) + half, F32),
            pltpu.VMEM((2, 4) + half, F32),
            pltpu.VMEM((2, 4) + half, F32),
            pltpu.VMEM((columns, 24, BLK * BLK, BLK * LY), F32),
            pltpu.VMEM((128, 128), F32),
            pltpu.VMEM((CITERS,) + tile, F32),
            pltpu.VMEM(tile, F32),
            pltpu.VMEM((CITERS - 1, 6) + tile, F32),
            pltpu.VMEM((columns, 2, nv, 8, nv), F32),
            pltpu.VMEM((128, 128), F32),
            pltpu.SemaphoreType.DMA((8,)),
            pltpu.SemaphoreType.DMA((n_copies,)),
            pltpu.SemaphoreType.DMA((n_copies,)),
        ],
        compiler_params=pltpu.CompilerParams(
            collective_id=0, has_side_effects=True, vmem_limit_bytes=67_043_328
        ),
    )(
        bc_sign,
        block_slot.reshape(-1),
        source.reshape(spinor),
        iterate.reshape(spinor),
        gauge_links.reshape(gauge_shape),
        clover.reshape(clover_shape),
        null_store.reshape(nulls),
        links,
    )
    outs = pl.pallas_call(
        hand_over,
        out_shape=(fine, fine),
        in_specs=[hbm, hbm],
        out_specs=(pl.BlockSpec(memory_space=pltpu.HBM),) * 2,
        scratch_shapes=[pltpu.VMEM(spinor, F32), pltpu.VMEM(spinor, F32), pltpu.SemaphoreType.DMA((4,))],
        compiler_params=pltpu.CompilerParams(vmem_limit_bytes=67_043_328),
    )(*outs)
    return tuple(out.reshape(source.shape) for out in outs)


def solution(mesh):
    placed = (
        P(None, None, None, "ta", "gz", "xy"),
        P(None, None, None, "ta", "gz", "xy"),
        P(None, None, None, None, "ta", "gz", "xy"),
        P(None, None, None, None, "ta", "gz", "xy"),
        P(),
        P("ta", "gz", "xy", None, None, None, None, None, None),
        P("ta", "gz", "xy"),
        P(None, None, None, None, "ta", "gz", "xy", None),
    )
    return jax.shard_map(
        functools.partial(per_device, dict(mesh.shape)),
        mesh=mesh,
        in_specs=placed,
        out_specs=(P(None, None, None, "ta", "gz", "xy"), P(None, None, None, "ta", "gz", "xy")),
        check_vma=False,
    )
```

profile of v0, /device:TPU:0, one launch (start us, length us, event | category | flops | bytes accessed | tf_op | source)
XLA Modules:
  0.0 38.3 jit_solution(6859563473744996010)
XLA Ops:
  0.6 35.7 %shard_map.95 = (f32[24,4,8,128]{3,2,1,0:T(8,128)}, f32[24,4,8,128]{3,2,1,0:T(8,128)}) custom-call(s32[4]{0:T(128)} %bc_ref.1, s32[2]{0:T(128)} %bitcast.19, f32[24,4,8,128]{3,2,1,0:T(8,128)} %bitcast.17, f32[24,4,8,128]{3,2,1,0:T(8,128)} %bitcast.18, f32[4,2,9,4,8,128]{5,4,3,2,1,0:T(8,128)} %bitcast.16, f32[2,2,36,4,8,128]{5,4,3,2,1,0:T(8,128)} %bitcast.15, ...), custom_call_target="tpu_custom_call" | custom-call | tf_op jit(solution)/shard_map/pallas_call | solution.py:451
  36.4 1.9 %shard_map.96 = (f32[24,4,8,128]{3,2,1,0:T(8,128)}, f32[24,4,8,128]{3,2,1,0:T(8,128)}) custom-call(f32[24,4,8,128]{3,2,1,0:T(8,128)} %get-tuple-element.6.it_in, f32[24,4,8,128]{3,2,1,0:T(8,128)} %get-tuple-element.7.res_in), custom_call_target="tpu_custom_call" | custom-call | tf_op jit(solution)/shard_map/pallas_call | solution.py:496
where the time goes:
time: 38.4 us; the launch traced here: 38.3 us
  Pallas kernels  37.6 us (98%)
  between operations  0.64 us (2%)
    pallas_call x1, Pallas kernels, per_device(): pl.pallas_call(functools.partial(kernel, counts), out_shape=(fine, fine),...  35.7 us
    pallas_call x1, Pallas kernels, per_device(): pl.pallas_call(hand_over, out_shape=(fine, fine), in_specs=[hbm, hbm], ou...  1.91 us

commit v1 on v0

v1 whole, which is shorter than its diff:
```python
import functools

import jax
import jax.numpy as jnp
from jax import lax
from jax.experimental import pallas as pl
from jax.experimental.pallas import tpu as pltpu
from jax.sharding import PartitionSpec as P

BLK = 4
LY = 32
CITERS = 4
MASS_TERM = 3.8
RELAX_WEIGHT = 0.4
HIGHEST = lax.Precision.HIGHEST
MESH = pl.DeviceIdType.MESH
LANES = 32
F32 = jnp.float32

UPPER = [((0, 0), (1, 0)), ((0, 3), (1, 1)), ((1, 3), (0, 3)), ((1, 2), (0, 0))]
LOWER = [((0, 0), (1, 0)), ((0, 1), (1, 3)), ((1, 1), (0, 1)), ((1, 0), (0, 2))]


def add_turned(a, b, power):
    power %= 4
    if power == 0:
        return (a[0] + b[0], a[1] + b[1])
    if power == 1:
        return (a[0] - b[1], a[1] + b[0])
    if power == 2:
        return (a[0] - b[0], a[1] - b[1])
    return (a[0] + b[1], a[1] - b[0])


def project(psi, mu, forward):
    turn = 2 if forward else 0
    return [
        [add_turned(psi[row][c], psi[2 + UPPER[mu][row][0]][c], UPPER[mu][row][1] + turn) for c in range(3)]
        for row in range(2)
    ]


def rebuild(total, half, mu, forward):
    turn = 2 if forward else 0
    for row in range(2):
        index, power = LOWER[mu][row]
        for c in range(3):
            total[row][c] = add_turned(total[row][c], half[row][c], 0)
            total[2 + row][c] = add_turned(total[2 + row][c], half[index][c], power + turn)


def link_times(link, half):
    out = [[None] * 3 for _ in range(2)]
    for a in range(3):
        for b in range(3):
            ur, ui = link(0, a * 3 + b), link(1, a * 3 + b)
            for s in range(2):
                hr, hi = half[s][b]
                term = (ur * hr - ui * hi, ur * hi + ui * hr)
                out[s][a] = term if b == 0 else add_turned(out[s][a], term, 0)
    return out


def link_dagger(link, half):
    out = [[None] * 3 for _ in range(2)]
    for a in range(3):
        for b in range(3):
            ur, ui = link(0, b * 3 + a), link(1, b * 3 + a)
            for s in range(2):
                hr, hi = half[s][b]
                term = (ur * hr + ui * hi, ur * hi - ui * hr)
                out[s][a] = term if b == 0 else add_turned(out[s][a], term, 0)
    return out


def rows(ref, index, height=8):
    start = index * height
    return ref[pl.ds(start if isinstance(index, int) else pl.multiple_of(start, height), height), :]


def put_rows(ref, index, value, height=8):
    start = index * height
    ref[pl.ds(start if isinstance(index, int) else pl.multiple_of(start, height), height), :] = value


def spinor_of(get):
    return [[(get(s * 3 + c), get(12 + s * 3 + c)) for c in range(3)] for s in range(4)]


def half_of(get):
    return [[(get(s * 3 + c), get(6 + s * 3 + c)) for c in range(3)] for s in range(2)]


def put_half(half, put):
    for s in range(2):
        for c in range(3):
            put(s * 3 + c, half[s][c][0])
            put(6 + s * 3 + c, half[s][c][1])


def map_half(half, change):
    return [[(change(z[0]), change(z[1])) for z in row] for row in half]


def zero_spinor(like):
    return [[(jnp.zeros_like(like), jnp.zeros_like(like)) for _ in range(3)] for _ in range(4)]


def roll(value, shift, axis):
    shift %= value.shape[axis]
    return value if shift == 0 else pltpu.roll(value, shift, axis)


def split_columns(a, b, top):
    return (
        jnp.where(top, a, pltpu.roll(b, BLK, 0)),
        jnp.where(top, pltpu.roll(a, BLK, 0), b),
    )


def wide(a, b):
    return a.astype(F32) * b.astype(F32)


def kernel(
    counts, bc_hbm, slot_hbm, src_hbm, it_hbm, ga_hbm, cl_hbm, nu_hbm, co_hbm, out_it, out_res,
    bc_ref, slot_ref, src, itv, ga, cl, nu, co, res, corr, gx, st, sx, sz, rt, rx, rz, hx, fc, red, pk, part, wbuf,
    wr, rhs, wexp, wv, pc, load_sem, send_sem, recv_sem,
):
    T = BLK
    names = ("ta", "gz", "xy")
    nv = nu.shape[2]

    def load(number, source, target):
        copy = pltpu.make_async_copy(source, target, load_sem.at[number])
        copy.start()
        return copy

    def link_part(ref, mu):
        size = ref.shape[0] // 4
        return ref.at[pl.ds(mu * size, size), :]

    load_it = load(0, it_hbm, itv)
    load_x = load(1, link_part(ga_hbm, 2), link_part(ga, 2))
    place = {n: lax.axis_index(n) for n in names}
    ahead = {n: {n: lax.rem(place[n] + 1, counts[n])} for n in names}
    behind = {n: {n: lax.rem(place[n] + counts[n] - 1, counts[n])} for n in names}
    barrier = pltpu.get_barrier_semaphore()
    for n in ("xy", "ta", "gz"):
        for target in (ahead[n], behind[n]):
            pl.semaphore_signal(barrier, inc=1, device_id=target, device_id_type=MESH)
    load_t = load(2, link_part(ga_hbm, 0), link_part(ga, 0))
    load_z = load(3, link_part(ga_hbm, 1), link_part(ga, 1))
    load_bc = load(4, bc_hbm, bc_ref)
    load_slot = load(5, slot_hbm, slot_ref)
    load_y = load(6, link_part(ga_hbm, 3), link_part(ga, 3))
    load_src = load(7, src_hbm, src)
    load_cl = load(8, cl_hbm, cl)
    load_co = load(9, co_hbm, co)
    load_nu = load(10, nu_hbm, nu)

    def send(phase, number, source, target, device):
        slot = (phase % 2) * 6 + number
        copy = pltpu.make_async_remote_copy(
            src_ref=source, dst_ref=target, send_sem=send_sem.at[slot], recv_sem=recv_sem.at[slot],
            device_id=device, device_id_type=MESH,
        )
        copy.start()
        return copy

    row = lax.broadcasted_iota(jnp.int32, (8, 128), 0)
    lane = lax.broadcasted_iota(jnp.int32, (8, 128), 1)
    column_y = lane & (LY - 1)
    group = lane // LY
    top = row < BLK

    def gauge(mu, t):
        return lambda ri, m: rows(ga, ((mu * 2 + ri) * 9 + m) * T + t)

    def gauge_edge_z(ri, m):
        return ga[pl.ds((((2 + ri) * 9 + m) * T) * 8 + 7, T, stride=8), :]

    def gauge_edge_x(ri, m):
        return rows(gx, ri * 9 + m)

    def site(field, t):
        return spinor_of(lambda k: rows(field, k * T + t))

    def gathered(values, offset):
        moved = [roll(v, LY * t + offset, 1) for t, v in enumerate(values)]
        value = moved[T - 1]
        for t in range(T - 1):
            value = jnp.where(group == t, moved[t], value)
        return value

    def pack_links(ri, carry):
        for m in range(9):
            base = (((4 + ri) * 9 + m) * T)
            put_rows(gx, ri * 9 + m, gathered([rows(ga, base + t) for t in range(T)], LY))
        return carry

    def send_x(d, field):
        sites = [site(field, t) for t in range(T)]
        first_half = [project(psi, 2, True) for psi in sites]
        last_half = [project(psi, 2, False) for psi in sites]

        def joined(halves, offset):
            return [
                [tuple(gathered([h[s][c][ri] for h in halves], offset) for ri in range(2)) for c in range(3)]
                for s in range(2)
            ]

        put_half(joined(first_half, 0), lambda c, v: put_rows(sx.at[d, 0], c, v))
        copy_0 = send(d * 4, 0, sx.at[d, 0], rx.at[d, 0], behind["xy"])
        put_half(link_dagger(gauge_edge_x, joined(last_half, LY)), lambda c, v: put_rows(sx.at[d, 1], c, v))
        copy_1 = send(d * 4, 1, sx.at[d, 1], rx.at[d, 1], ahead["xy"])
        return [copy_0, copy_1]

    def send_t(d, field):
        put_half(project(site(field, 0), 0, True), lambda c, v: put_rows(st.at[d, 0], c, v))
        copy_0 = send(d * 4, 2, st.at[d, 0], rt.at[d, 0], behind["ta"])
        half = link_dagger(gauge(0, T - 1), project(site(field, T - 1), 0, False))
        put_half(half, lambda c, v: put_rows(st.at[d, 1], c, v))
        copy_1 = send(d * 4, 3, st.at[d, 1], rt.at[d, 1], ahead["ta"])
        return [copy_0, copy_1]

    def send_z(d, field):
        low = spinor_of(lambda k: field[pl.ds(k * T * 8, T, stride=8), :])
        put_half(project(low, 1, True), lambda c, v: put_rows(sz.at[d, 0], c, v, T))
        copy_0 = send(d * 4, 4, sz.at[d, 0], rz.at[d, 0], behind["gz"])
        high = spinor_of(lambda k: field[pl.ds(k * T * 8 + 7, T, stride=8), :])
        half = link_dagger(gauge_edge_z, project(high, 1, False))
        put_half(half, lambda c, v: put_rows(sz.at[d, 1], c, v, T))
        copy_1 = send(d * 4, 5, sz.at[d, 1], rz.at[d, 1], ahead["gz"])
        return [copy_0, copy_1]

    def local_part(field, base, out, sign_y):
        def body(t, carry):
            psi = site(field, t)
            total = zero_spinor(psi[0][0][0])

            def up(v):
                return jnp.where(column_y == LY - 1, roll(v, LY - 1, 1) * sign_y, roll(v, -1, 1))

            def down(v):
                return jnp.where(column_y == 0, roll(v, 1 - LY, 1) * sign_y, roll(v, 1, 1))

            rebuild(total, link_times(gauge(3, t), map_half(project(psi, 3, True), up)), 3, True)
            rebuild(total, map_half(link_dagger(gauge(3, t), project(psi, 3, False)), down), 3, False)
            inner = map_half(project(psi, 2, True), lambda v: jnp.where(lane >= 128 - LY, 0.0, roll(v, -LY, 1)))
            rebuild(total, link_times(gauge(2, t), inner), 2, True)
            inner = link_dagger(gauge(2, t), project(psi, 2, False))
            rebuild(total, map_half(inner, lambda v: jnp.where(lane < LY, 0.0, roll(v, LY, 1))), 2, False)
            inner = map_half(project(psi, 1, True), lambda v: jnp.where(row == 7, 0.0, roll(v, -1, 0)))
            rebuild(total, link_times(gauge(1, t), inner), 1, True)
            inner = link_dagger(gauge(1, t), project(psi, 1, False))
            rebuild(total, map_half(inner, lambda v: jnp.where(row == 0, 0.0, roll(v, 1, 0))), 1, False)
            next_t, last_t = lax.rem(t + 1, T), lax.rem(t + T - 1, T)
            inside = jnp.where(t == T - 1, 0.0, 1.0)
            inner = link_times(gauge(0, t), project(site(field, next_t), 0, True))
            rebuild(total, map_half(inner, lambda v: v * inside), 0, True)
            within = jnp.where(t == 0, 0.0, 1.0)
            inner = link_dagger(gauge(0, last_t), project(site(field, last_t), 0, False))
            rebuild(total, map_half(inner, lambda v: v * within), 0, False)
            for ch in range(2):
                for i in range(6):
                    s, c = 2 * ch + i // 3, i % 3
                    re, im = psi[s][c][0] * MASS_TERM, psi[s][c][1] * MASS_TERM
                    for j in range(6):
                        vr, vi = psi[2 * ch + j // 3][j % 3]
                        index = (ch * 2 * 36 + i * 6 + j) * T + t
                        mr, mi = rows(cl, index), rows(cl, index + 36 * T)
                        re = re + (mr * vr - mi * vi)
                        im = im + (mr * vi + mi * vr)
                    k = s * 3 + c
                    here, there = k * T + t, (12 + k) * T + t
                    put_rows(out, here, rows(base, here) - re + 0.5 * total[s][c][0])
                    put_rows(out, there, rows(base, there) - im + 0.5 * total[s][c][1])
            return carry

        lax.fori_loop(0, T, body, 0)

    def add_to(out, total, where):
        for s in range(4):
            for c in range(3):
                for ri in range(2):
                    spot = where(ri * 12 + s * 3 + c)
                    out[spot] = out[spot] + 0.5 * total[s][c][ri]

    def far_part(d, out, copies, last, first):
        copies[4].wait()
        copies[5].wait()
        edge = half_of(lambda c: rows(rz.at[d, 0], c, T) * last[1])
        total = zero_spinor(edge[0][0][0])
        rebuild(total, link_times(gauge_edge_z, edge), 1, True)
        add_to(out, total, lambda k: (pl.ds(k * T * 8 + 7, T, stride=8), slice(None)))
        total = zero_spinor(edge[0][0][0])
        rebuild(total, half_of(lambda c: rows(rz.at[d, 1], c, T) * first[1]), 1, False)
        add_to(out, total, lambda k: (pl.ds(k * T * 8, T, stride=8), slice(None)))
        copies[2].wait()
        copies[3].wait()
        total = zero_spinor(lane.astype(F32))
        edge = half_of(lambda c: rows(rt.at[d, 0], c) * last[0])
        rebuild(total, link_times(gauge(0, T - 1), edge), 0, True)
        add_to(out, total, lambda k: (pl.ds((k * T + T - 1) * 8, 8), slice(None)))
        total = zero_spinor(lane.astype(F32))
        rebuild(total, half_of(lambda c: rows(rt.at[d, 1], c) * first[0]), 0, False)
        add_to(out, total, lambda k: (pl.ds(k * T * 8, 8), slice(None)))
        copies[1].wait()
        copies[0].wait()
        edge = half_of(lambda c: rows(rx.at[d, 0], c) * last[2])
        put_half(link_times(gauge_edge_x, edge), lambda c, v: put_rows(hx, c, v))
        way = jnp.where(group == T - 1, -1.0, 1.0)
        for t in range(T):
            def both(c):
                fore = roll(rows(hx, c), -LY * (t + 1), 1)
                back = roll(rows(rx.at[d, 1], c) * first[2], -LY * t, 1)
                return jnp.where(group == T - 1, fore, jnp.where(group == 0, back, 0.0))

            half = half_of(both)
            total = zero_spinor(lane.astype(F32))
            for s in range(2):
                index, power = LOWER[2][s]
                for c in range(3):
                    total[s][c] = half[s][c]
                    z = half[index][c]
                    total[2 + s][c] = add_turned(total[2 + s][c], (z[0] * way, z[1] * way), power)
            add_to(out, total, lambda k: (pl.ds((k * T + t) * 8, 8), slice(None)))

    load_x.wait()
    lax.fori_loop(0, 2, pack_links, 0)
    load_it.wait()
    pl.semaphore_wait(barrier, 6)
    copies = send_x(0, itv)
    load_t.wait()
    copies += send_t(0, itv)
    load_z.wait()
    copies += send_z(0, itv)
    load_bc.wait()
    load_slot.wait()
    sign = [bc_ref[mu].astype(F32) for mu in range(4)]
    last = [jnp.where(place[n] == counts[n] - 1, sign[i], 1.0) for i, n in enumerate(names)]
    first = [jnp.where(place[n] == 0, sign[i], 1.0) for i, n in enumerate(names)]
    swap = jnp.full((8, 128), slot_ref[0], jnp.int32) != 0
    load_y.wait()
    load_src.wait()
    load_cl.wait()
    local_part(itv, src, res, sign[3])
    load_co.wait()

    def pack_coarse(i, carry):
        for k in range(9):
            parts = []
            for col in range(2):
                for ri in range(2):
                    parts.append(jnp.concatenate([co[k, ri, i, col], jnp.zeros((8, 128 - nv), F32)], axis=1))
            value = parts[0]
            for g in range(1, 4):
                value = jnp.where(group == g, roll(parts[g], LANES * g, 1), value)
            pk[k, i] = value
        return carry

    lax.fori_loop(0, nv, pack_coarse, 0)
    far_part(0, res, copies, last, first)

    def to_columns(k, carry):
        low, high = [], []
        for pair, group_of in enumerate((low, high)):
            a, b = rows(res, k * T + 2 * pair), rows(res, k * T + 2 * pair + 1)
            col_0, col_1 = split_columns(a, b, top)
            group_of.append(jnp.where(swap, col_1, col_0))
            group_of.append(jnp.where(swap, col_0, col_1))
        for slot in range(2):
            value = jnp.concatenate([low[slot], high[slot]], axis=0).astype(jnp.bfloat16)
            fc[slot, k] = value
            fc[slot, 24 + k] = -value
        return carry

    lax.fori_loop(0, 24, to_columns, 0)
    load_nu.wait()
    red[...] = jnp.zeros(red.shape, F32)
    for slot in range(2):
        def restrict(g, carry):
            sums = [None] * 4
            for s in range(12):
                fr, fi, minus = fc[slot, s], fc[slot, 12 + s], fc[slot, 24 + s]
                for j in range(2):
                    nr, ni = nu[slot, 0, g * 2 + j, s], nu[slot, 1, g * 2 + j, s]
                    for q, pair in enumerate(((fr, fi), (fi, minus))):
                        at = 2 * j + q
                        term = wide(nr, pair[0])
                        sums[at] = term if sums[at] is None else sums[at] + term
                        sums[at] = sums[at] + wide(ni, pair[1])
            for j in range(2):
                for ri in range(2):
                    value = sums[2 * j + ri]
                    put_rows(red, (2 * slot + ri) * LANES + g * 2 + j, value[:8] + value[8:])
            return carry

        lax.fori_loop(0, nv // 2, restrict, 0)
    chooser = ((column_y // BLK) == row).astype(F32)
    gathered_rows = red[pl.ds(0, 128, stride=8), :]
    for r in range(1, 8):
        gathered_rows = gathered_rows + red[pl.ds(r, 128, stride=8), :]
    value = lax.dot_general(
        chooser, gathered_rows, (((1,), (1,)), ((), ())), precision=HIGHEST, preferred_element_type=F32
    )
    value = jnp.where(swap, roll(value, 2 * LANES, 1), value)
    rhs[...] = value
    wbuf[0] = RELAX_WEIGHT * value

    even = (group & 1) == 0
    turn = jnp.where(even, 1.0, -1.0)

    def pairs_of(w):
        return w * turn, jnp.where(even, roll(w, -LANES, 1), roll(w, LANES, 1))

    def products(vectors, i, sums):
        for k, (wa, wb) in vectors:
            y = pk[k, i]
            sums = (y * wa, y * wb) if sums is None else (sums[0] + y * wa, sums[1] + y * wb)
        return sums

    block = 8
    for it in range(CITERS - 1):
        phase = it + 1
        own = wbuf[it]
        targets = [behind["xy"], ahead["xy"], behind["ta"], ahead["ta"], behind["gz"], ahead["gz"]]
        copies = [send(phase, d, wbuf.at[it], wr.at[it, d], targets[d]) for d in range(6)]
        vectors = [(0, pairs_of(own)), (7, pairs_of(roll(own, -1, 0))), (8, pairs_of(roll(own, 1, 0)))]

        def near(g, carry):
            for j in range(block):
                i = g * block + j
                part[0, i], part[1, i] = products(vectors, i, None)
            return carry

        lax.fori_loop(0, nv // block, near, 0)
        copies[4].wait()
        copies[5].wait()
        half = 2 * LANES
        next_z = jnp.where(lane < half, roll(own, half, 1), roll(wr[it, 4], half, 1))
        last_z = jnp.where(lane < half, roll(wr[it, 5], half, 1), roll(own, half, 1))
        z_vectors = [(3, pairs_of(next_z)), (4, pairs_of(last_z))]

        def middle(g, carry):
            for j in range(block):
                i = g * block + j
                part[0, i], part[1, i] = products(z_vectors, i, (part[0, i], part[1, i]))
            return carry

        lax.fori_loop(0, nv // block, middle, 0)
        for d in range(4):
            copies[d].wait()
        far_vectors = [(k, pairs_of(wr[it, d])) for k, d in ((1, 2), (2, 3), (5, 0), (6, 1))]
        applied = jnp.zeros((8, 128), F32)
        for i in range(nv):
            sums = products(far_vectors, i, (part[0, i], part[1, i]))
            for ri in range(2):
                for col in range(2):
                    mine = (lane < half) if col == 0 else (lane >= half)
                    whole = jnp.sum(jnp.where(mine, sums[ri], 0.0), axis=1, keepdims=True)
                    applied = jnp.where(lane == LANES * (2 * col + ri) + i, whole, applied)
        wbuf[it + 1] = own + RELAX_WEIGHT * (rhs[...] - (2.0 * own + applied))

    w = wbuf[CITERS - 1]
    w = jnp.where(swap, roll(w, 2 * LANES, 1), w).astype(jnp.bfloat16)
    wexp[...] = lax.dot_general(
        w, chooser.astype(jnp.bfloat16), (((0,), (0,)), ((), ())), preferred_element_type=F32
    )

    def spread(c, carry):
        for slot in range(2):
            values = [wexp[pl.ds((2 * slot + ri) * LANES + c, 1), :] for ri in range(2)]
            for at, v in enumerate((values[0], values[1], -values[1])):
                wv[slot, at, c] = jnp.broadcast_to(v, (2 * 8, 128)).astype(jnp.bfloat16)
        return carry

    lax.fori_loop(0, nv, spread, 0)
    for slot in range(2):
        def prolong(q, carry):
            sums = [None] * 4
            for c in range(nv):
                vr, vi, minus = wv[slot, 0, c], wv[slot, 1, c], wv[slot, 2, c]
                for j in range(2):
                    nr, ni = nu[slot, 0, c, q * 2 + j], nu[slot, 1, c, q * 2 + j]
                    for ri, pair in enumerate(((vr, minus), (vi, vr))):
                        at = 2 * j + ri
                        term = wide(nr, pair[0])
                        sums[at] = term if sums[at] is None else sums[at] + term
                        sums[at] = sums[at] + wide(ni, pair[1])
            for j in range(2):
                for ri in range(2):
                    pc[slot, ri * 12 + q * 2 + j] = sums[2 * j + ri]
            return carry

        lax.fori_loop(0, 6, prolong, 0)

    def from_columns(k, carry):
        for pair in range(2):
            part_0, part_1 = pc[0, k, pl.ds(8 * pair, 8), :], pc[1, k, pl.ds(8 * pair, 8), :]
            part_0, part_1 = jnp.where(swap, part_1, part_0), jnp.where(swap, part_0, part_1)
            for h, value in enumerate(split_columns(part_0, part_1, top)):
                at = k * T + 2 * pair + h
                put_rows(corr, at, value)
                put_rows(out_it, at, rows(itv, at) + value)
        return carry

    lax.fori_loop(0, 24, from_columns, 0)
    copies = send_x(1, corr) + send_t(1, corr) + send_z(1, corr)
    local_part(corr, res, out_res, sign[3])
    far_part(1, out_res, copies, last, first)


def hand_over(it_in, res_in, it_out, res_out, sem):
    copies = [
        pltpu.make_async_copy(a, b, sem.at[i]) for i, (a, b) in enumerate(((it_in, it_out), (res_in, res_out)))
    ]
    for copy in copies:
        copy.start()
    for copy in copies:
        copy.wait()


def per_device(counts, source, iterate, gauge_links, clover, bc_sign, null_store, block_slot, coarse_links):
    lattice = source.shape[3:]
    T = lattice[0]
    columns = block_slot.size
    nv = null_store.shape[4]
    assert lattice == (BLK, 2 * BLK, BLK * LY) and columns == 2 and nv % 8 == 0 and nv <= LANES
    nulls = (columns,) + null_store.shape[3:6] + (BLK * BLK, BLK * LY)
    links = jnp.transpose(coarse_links, (0, 1, 2, 4, 5, 6, 7, 3))
    links = links.reshape(links.shape[:3] + (columns,) + links.shape[6:])
    tall = T * lattice[1]
    field = (24 * tall, lattice[2])
    half = 12 * lattice[1]
    tile = lattice[1:]
    hbm = pl.BlockSpec(memory_space=pltpu.HBM)
    vmem = pl.BlockSpec(memory_space=pltpu.VMEM)
    outs = pl.pallas_call(
        functools.partial(kernel, counts),
        out_shape=(pltpu.VMEM(field, F32),) * 2,
        in_specs=[hbm] * 8,
        out_specs=(vmem,) * 2,
        scratch_shapes=[
            pltpu.SMEM(bc_sign.shape, jnp.int32),
            pltpu.SMEM((columns,), jnp.int32),
            pltpu.VMEM(field, F32),
            pltpu.VMEM(field, F32),
            pltpu.VMEM((72 * tall, 128), F32),
            pltpu.VMEM((144 * tall, 128), F32),
            pltpu.VMEM(nulls, jnp.bfloat16),
            pltpu.VMEM(links.shape, F32),
            pltpu.VMEM(field, F32),
            pltpu.VMEM(field, F32),
            pltpu.VMEM((18 * 8, 128), F32),
            pltpu.VMEM((2, 2, half, 128), F32),
            pltpu.VMEM((2, 2, half, 128), F32),
            pltpu.VMEM((2, 2, 12 * T, 128), F32),
            pltpu.VMEM((2, 2, half, 128), F32),
            pltpu.VMEM((2, 2, half, 128), F32),
            pltpu.VMEM((2, 2, 12 * T, 128), F32),
            pltpu.VMEM((half, 128), F32),
            pltpu.VMEM((columns, 48, BLK * BLK, 128), jnp.bfloat16),
            pltpu.VMEM((128 * 8, 128), F32),
            pltpu.VMEM((9, nv) + tile, F32),
            pltpu.VMEM((2, nv) + tile, F32),
            pltpu.VMEM((CITERS,) + tile, F32),
            pltpu.VMEM((CITERS - 1, 6) + tile, F32),
            pltpu.VMEM(tile, F32),
            pltpu.VMEM((128, 128), F32),
            pltpu.VMEM((columns, 3, nv, BLK * BLK, 128), jnp.bfloat16),
            pltpu.VMEM((columns, 24, BLK * BLK, 128), F32),
            pltpu.SemaphoreType.DMA((11,)),
            pltpu.SemaphoreType.DMA((12,)),
            pltpu.SemaphoreType.DMA((12,)),
        ],
        compiler_params=pltpu.CompilerParams(
            collective_id=0, has_side_effects=True, vmem_limit_bytes=66_200_000
        ),
    )(
        bc_sign,
        block_slot.reshape(-1),
        source.reshape(field),
        iterate.reshape(field),
        gauge_links.reshape(72 * tall, 128),
        clover.reshape(144 * tall, 128),
        null_store.reshape(nulls),
        links,
    )
    outs = pl.pallas_call(
        hand_over,
        out_shape=(jax.ShapeDtypeStruct(field, F32),) * 2,
        in_specs=[pl.BlockSpec(memory_space=pl.ANY)] * 2,
        out_specs=(hbm,) * 2,
        scratch_shapes=[pltpu.SemaphoreType.DMA((2,))],
        compiler_params=pltpu.CompilerParams(vmem_limit_bytes=66_200_000),
    )(*outs)
    return tuple(out.reshape(source.shape) for out in outs)


def solution(mesh):
    placed = (
        P(None, None, None, "ta", "gz", "xy"),
        P(None, None, None, "ta", "gz", "xy"),
        P(None, None, None, None, "ta", "gz", "xy"),
        P(None, None, None, None, "ta", "gz", "xy"),
        P(),
        P("ta", "gz", "xy", None, None, None, None, None, None),
        P("ta", "gz", "xy"),
        P(None, None, None, None, "ta", "gz", "xy", None),
    )
    return jax.shard_map(
        functools.partial(per_device, dict(mesh.shape)),
        mesh=mesh,
        in_specs=placed,
        out_specs=(P(None, None, None, "ta", "gz", "xy"), P(None, None, None, "ta", "gz", "xy")),
        check_vma=False,
    )
```

time: 38.4 us -> 56.6 us (1.47)
  Pallas kernels: 37.6 us -> 54.3 us
  local copies, waits for them, and re-layouts: 0 us -> 1.49 us
    pallas_call x2, Pallas kernels: 37.6 us -> 54.3 us  [the longest x1 29.4 us: per_device(): pl.pallas_call(functools.partial(kernel, counts), out_shape=(pltpu.VMEM(f...]
    unnamed x0 -> x4, local copies, waits for them, and re-layouts: none -> 1.49 us
where the time goes in v1:
time: 56.6 us; the launch traced here: 56.4 us
  Pallas kernels  54.3 us (96%)
  local copies, waits for them, and re-layouts  1.49 us (3%)
  between operations  0.65 us (1%)
    pallas_call x1, Pallas kernels, per_device(): pl.pallas_call(functools.partial(kernel, counts), out_shape=(pltpu.VMEM(f...  29.4 us
    pallas_call x1, Pallas kernels, per_device(): pl.pallas_call(hand_over, out_shape=(jax.ShapeDtypeStruct(field, F32),) *...  24.9 us
    unnamed x4, local copies, waits for them, and re-layouts  1.49 us

profile of v1, /device:TPU:0, one launch (start us, length us, event | category | flops | bytes accessed | tf_op | source)
XLA Modules:
  0.0 56.4 jit_solution(18355196837721650013)
XLA Ops:
  0.6 29.4 %shard_map.95 = (f32[768,128]{1,0:T(8,128)S(1)}, f32[768,128]{1,0:T(8,128)S(1)}) custom-call(s32[4]{0:T(128)} %bc_hbm.1, s32[2]{0:T(128)} %bitcast.19, f32[768,128]{1,0:T(8,128)} %bitcast.17, f32[768,128]{1,0:T(8,128)} %bitcast.18, f32[2304,128]{1,0:T(8,128)} %bitcast.16, f32[4608,128]{1,0:T(8,128)} %bitcast.15, bf16[2,2,24,12,16,128]{5,4,3,2,1,0:T(8,128)(2,1)} %bitcast.13, ...), custom_call_target="tpu_custom_call" | custom-call | tf_op jit(solution)/shard_map/pallas_call | solution.py:540
  30.0 0.0 copy-start
  30.0 0.7 %copy-done = f32[768,128]{1,0:T(8,128)} copy-done((f32[768,128]{1,0:T(8,128)}, f32[768,128]{1,0:T(8,128)S(1)}, u32[]{:S(2)}) %copy-start) | copy-done | bytes 393240
  30.7 0.0 copy-start.1
  30.7 0.7 %copy-done.1 = f32[768,128]{1,0:T(8,128)} copy-done((f32[768,128]{1,0:T(8,128)}, f32[768,128]{1,0:T(8,128)S(1)}, u32[]{:S(2)}) %copy-start.1) | copy-done | bytes 393240
  31.5 24.9 %shard_map.96 = (f32[768,128]{1,0:T(8,128)}, f32[768,128]{1,0:T(8,128)}) custom-call(f32[768,128]{1,0:T(8,128)} %copy-done, f32[768,128]{1,0:T(8,128)} %copy-done.1), custom_call_target="tpu_custom_call" | custom-call | tf_op jit(solution)/shard_map/pallas_call | solution.py:591
Async XLA Ops:
  30.0 0.8 %copy-start = (f32[768,128]{1,0:T(8,128)}, f32[768,128]{1,0:T(8,128)S(1)}, u32[]{:S(2)}) copy-start(f32[768,128]{1,0:T(8,128)S(1)} %get-tuple-element.6.it_in) | copy-start | bytes 1179652
  30.7 0.7 %copy-start.1 = (f32[768,128]{1,0:T(8,128)}, f32[768,128]{1,0:T(8,128)S(1)}, u32[]{:S(2)}) copy-start(f32[768,128]{1,0:T(8,128)S(1)} %get-tuple-element.7.res_in) | copy-start | bytes 1179652

commit v2 on v1

--- a/solution.py
+++ b/solution.py
@@ -12,7 +12,6 @@
 CITERS = 4
 MASS_TERM = 3.8
 RELAX_WEIGHT = 0.4
-HIGHEST = lax.Precision.HIGHEST
 MESH = pl.DeviceIdType.MESH
 LANES = 32
 F32 = jnp.float32
@@ -199,54 +198,63 @@
             put_rows(gx, ri * 9 + m, gathered([rows(ga, base + t) for t in range(T)], LY))
         return carry
 
-    def send_x(d, field):
+    def ordered(d, number, name, outgoing, incoming, choice):
+        copies = [None, None]
+        for turn in range(2):
+            way = choice if turn == 0 else 1 - choice
+            target = {name: lax.rem(place[name] + counts[name] - 1 + 2 * way, counts[name])}
+            copies[turn] = send(d * 4, number + way, outgoing.at[d, way], incoming.at[d, way], target)
+        return copies
+
+    def fill_x(d, field):
         sites = [site(field, t) for t in range(T)]
-        first_half = [project(psi, 2, True) for psi in sites]
-        last_half = [project(psi, 2, False) for psi in sites]
-
-        def joined(halves, offset):
+
+        def joined(forward, offset):
+            halves = [project(psi, 2, forward) for psi in sites]
             return [
                 [tuple(gathered([h[s][c][ri] for h in halves], offset) for ri in range(2)) for c in range(3)]
                 for s in range(2)
             ]
 
-        put_half(joined(first_half, 0), lambda c, v: put_rows(sx.at[d, 0], c, v))
-        copy_0 = send(d * 4, 0, sx.at[d, 0], rx.at[d, 0], behind["xy"])
-        put_half(link_dagger(gauge_edge_x, joined(last_half, LY)), lambda c, v: put_rows(sx.at[d, 1], c, v))
-        copy_1 = send(d * 4, 1, sx.at[d, 1], rx.at[d, 1], ahead["xy"])
-        return [copy_0, copy_1]
-
-    def send_t(d, field):
+        put_half(joined(True, 0), lambda c, v: put_rows(sx.at[d, 0], c, v))
+        put_half(link_dagger(gauge_edge_x, joined(False, LY)), lambda c, v: put_rows(sx.at[d, 1], c, v))
+
+    def fill_t(d, field):
         put_half(project(site(field, 0), 0, True), lambda c, v: put_rows(st.at[d, 0], c, v))
-        copy_0 = send(d * 4, 2, st.at[d, 0], rt.at[d, 0], behind["ta"])
         half = link_dagger(gauge(0, T - 1), project(site(field, T - 1), 0, False))
         put_half(half, lambda c, v: put_rows(st.at[d, 1], c, v))
-        copy_1 = send(d * 4, 3, st.at[d, 1], rt.at[d, 1], ahead["ta"])
-        return [copy_0, copy_1]
-
-    def send_z(d, field):
+
+    def fill_z(d, field):
         low = spinor_of(lambda k: field[pl.ds(k * T * 8, T, stride=8), :])
         put_half(project(low, 1, True), lambda c, v: put_rows(sz.at[d, 0], c, v, T))
-        copy_0 = send(d * 4, 4, sz.at[d, 0], rz.at[d, 0], behind["gz"])
         high = spinor_of(lambda k: field[pl.ds(k * T * 8 + 7, T, stride=8), :])
         half = link_dagger(gauge_edge_z, project(high, 1, False))
         put_half(half, lambda c, v: put_rows(sz.at[d, 1], c, v, T))
-        copy_1 = send(d * 4, 5, sz.at[d, 1], rz.at[d, 1], ahead["gz"])
-        return [copy_0, copy_1]
-
-    def local_part(field, base, out, sign_y):
-        def body(t, carry):
+
+    def send_all(d, field, before):
+        before[0]()
+        fill_t(d, field)
+        copies_t = ordered(d, 2, "ta", st, rt, lax.rem(place["ta"], 2))
+        before[1]()
+        fill_x(d, field)
+        copies_x = ordered(d, 0, "xy", sx, rx, (place["xy"] + 1) // counts["xy"])
+        before[2]()
+        fill_z(d, field)
+        copies_z = ordered(d, 4, "gz", sz, rz, 0)
+        return copies_x + copies_t + copies_z
+
+    def local_part(field, base, out, sign_y, before):
+        def keep(total, t, old):
+            for s in range(4):
+                for c in range(3):
+                    for ri in range(2):
+                        at = (ri * 12 + s * 3 + c) * T + t
+                        value = 0.5 * total[s][c][ri]
+                        put_rows(out, at, rows(out, at) + value if old else value)
+
+        def inside_tile(t, carry):
             psi = site(field, t)
             total = zero_spinor(psi[0][0][0])
-
-            def up(v):
-                return jnp.where(column_y == LY - 1, roll(v, LY - 1, 1) * sign_y, roll(v, -1, 1))
-
-            def down(v):
-                return jnp.where(column_y == 0, roll(v, 1 - LY, 1) * sign_y, roll(v, 1, 1))
-
-            rebuild(total, link_times(gauge(3, t), map_half(project(psi, 3, True), up)), 3, True)
-            rebuild(total, map_half(link_dagger(gauge(3, t), project(psi, 3, False)), down), 3, False)
             inner = map_half(project(psi, 2, True), lambda v: jnp.where(lane >= 128 - LY, 0.0, roll(v, -LY, 1)))
             rebuild(total, link_times(gauge(2, t), inner), 2, True)
             inner = link_dagger(gauge(2, t), project(psi, 2, False))
@@ -255,6 +263,14 @@
             rebuild(total, link_times(gauge(1, t), inner), 1, True)
             inner = link_dagger(gauge(1, t), project(psi, 1, False))
             rebuild(total, map_half(inner, lambda v: jnp.where(row == 0, 0.0, roll(v, 1, 0))), 1, False)
+            keep(total, t, False)
+            return carry
+
+        lax.fori_loop(0, T, inside_tile, 0)
+        before[0]()
+
+        def along_t_y(t, carry):
+            total = zero_spinor(lane.astype(F32))
             next_t, last_t = lax.rem(t + 1, T), lax.rem(t + T - 1, T)
             inside = jnp.where(t == T - 1, 0.0, 1.0)
             inner = link_times(gauge(0, t), project(site(field, next_t), 0, True))
@@ -262,6 +278,24 @@
             within = jnp.where(t == 0, 0.0, 1.0)
             inner = link_dagger(gauge(0, last_t), project(site(field, last_t), 0, False))
             rebuild(total, map_half(inner, lambda v: v * within), 0, False)
+            psi = site(field, t)
+
+            def up(v):
+                return jnp.where(column_y == LY - 1, roll(v, LY - 1, 1) * sign_y, roll(v, -1, 1))
+
+            def down(v):
+                return jnp.where(column_y == 0, roll(v, 1 - LY, 1) * sign_y, roll(v, 1, 1))
+
+            rebuild(total, link_times(gauge(3, t), map_half(project(psi, 3, True), up)), 3, True)
+            rebuild(total, map_half(link_dagger(gauge(3, t), project(psi, 3, False)), down), 3, False)
+            keep(total, t, True)
+            return carry
+
+        lax.fori_loop(0, T, along_t_y, 0)
+        before[1]()
+
+        def on_site(t, carry):
+            psi = site(field, t)
             for ch in range(2):
                 for i in range(6):
                     s, c = 2 * ch + i // 3, i % 3
@@ -274,11 +308,11 @@
                         im = im + (mr * vi + mi * vr)
                     k = s * 3 + c
                     here, there = k * T + t, (12 + k) * T + t
-                    put_rows(out, here, rows(base, here) - re + 0.5 * total[s][c][0])
-                    put_rows(out, there, rows(base, there) - im + 0.5 * total[s][c][1])
+                    put_rows(out, here, rows(out, here) + rows(base, here) - re)
+                    put_rows(out, there, rows(out, there) + rows(base, there) - im)
             return carry
 
-        lax.fori_loop(0, T, body, 0)
+        lax.fori_loop(0, T, on_site, 0)
 
     def add_to(out, total, where):
         for s in range(4):
@@ -327,40 +361,39 @@
                     total[2 + s][c] = add_turned(total[2 + s][c], (z[0] * way, z[1] * way), power)
             add_to(out, total, lambda k: (pl.ds((k * T + t) * 8, 8), slice(None)))
 
-    load_x.wait()
-    lax.fori_loop(0, 2, pack_links, 0)
-    load_it.wait()
-    pl.semaphore_wait(barrier, 6)
-    copies = send_x(0, itv)
-    load_t.wait()
-    copies += send_t(0, itv)
-    load_z.wait()
-    copies += send_z(0, itv)
+    def ready_t():
+        load_it.wait()
+        load_t.wait()
+        pl.semaphore_wait(barrier, 6)
+
+    def ready_x():
+        load_x.wait()
+        lax.fori_loop(0, 2, pack_links, 0)
+
+    copies = send_all(0, itv, (ready_t, ready_x, load_z.wait))
     load_bc.wait()
     load_slot.wait()
     sign = [bc_ref[mu].astype(F32) for mu in range(4)]
     last = [jnp.where(place[n] == counts[n] - 1, sign[i], 1.0) for i, n in enumerate(names)]
     first = [jnp.where(place[n] == 0, sign[i], 1.0) for i, n in enumerate(names)]
     swap = jnp.full((8, 128), slot_ref[0], jnp.int32) != 0
-    load_y.wait()
-    load_src.wait()
-    load_cl.wait()
-    local_part(itv, src, res, sign[3])
-    load_co.wait()
-
-    def pack_coarse(i, carry):
-        for k in range(9):
-            parts = []
-            for col in range(2):
-                for ri in range(2):
-                    parts.append(jnp.concatenate([co[k, ri, i, col], jnp.zeros((8, 128 - nv), F32)], axis=1))
+
+    def ready_site():
+        load_src.wait()
+        load_cl.wait()
+
+    local_part(itv, src, res, sign[3], (load_y.wait, ready_site))
+
+    def pack_coarse(k, carry):
+        for i in range(nv):
+            parts = [co[k, ri, i, col] for col in range(2) for ri in range(2)]
+            parts = [jnp.concatenate([v, jnp.zeros((8, 128 - nv), F32)], axis=1) for v in parts]
             value = parts[0]
             for g in range(1, 4):
-                value = jnp.where(group == g, roll(parts[g], LANES * g, 1), value)
+                value = value + roll(parts[g], LANES * g, 1)
             pk[k, i] = value
         return carry
 
-    lax.fori_loop(0, nv, pack_coarse, 0)
     far_part(0, res, copies, last, first)
 
     def to_columns(k, carry):
@@ -398,13 +431,20 @@
             return carry
 
         lax.fori_loop(0, nv // 2, restrict, 0)
-    chooser = ((column_y // BLK) == row).astype(F32)
     gathered_rows = red[pl.ds(0, 128, stride=8), :]
     for r in range(1, 8):
         gathered_rows = gathered_rows + red[pl.ds(r, 128, stride=8), :]
-    value = lax.dot_general(
-        chooser, gathered_rows, (((1,), (1,)), ((), ())), precision=HIGHEST, preferred_element_type=F32
-    )
+    turned = jnp.transpose(gathered_rows)
+    value = None
+    for m in range(4):
+        part_sum = turned[8 * m:8 * m + 8]
+        for x in range(1, BLK):
+            part_sum = part_sum + turned[LY * x + 8 * m:LY * x + 8 * m + 8]
+        part_sum = part_sum + roll(part_sum, 1, 0)
+        part_sum = part_sum + roll(part_sum, 2, 0)
+        lower, upper = roll(part_sum, 2 * m - 3, 0), roll(part_sum, 2 * m + 1 - 7, 0)
+        here = jnp.where(row == 2 * m, lower, upper)
+        value = here if m == 0 else jnp.where(row // 2 == m, here, value)
     value = jnp.where(swap, roll(value, 2 * LANES, 1), value)
     rhs[...] = value
     wbuf[0] = RELAX_WEIGHT * value
@@ -427,6 +467,9 @@
         own = wbuf[it]
         targets = [behind["xy"], ahead["xy"], behind["ta"], ahead["ta"], behind["gz"], ahead["gz"]]
         copies = [send(phase, d, wbuf.at[it], wr.at[it, d], targets[d]) for d in range(6)]
+        if it == 0:
+            load_co.wait()
+            lax.fori_loop(0, 9, pack_coarse, 0)
         vectors = [(0, pairs_of(own)), (7, pairs_of(roll(own, -1, 0))), (8, pairs_of(roll(own, 1, 0)))]
 
         def near(g, carry):
@@ -464,10 +507,12 @@
         wbuf[it + 1] = own + RELAX_WEIGHT * (rhs[...] - (2.0 * own + applied))
 
     w = wbuf[CITERS - 1]
-    w = jnp.where(swap, roll(w, 2 * LANES, 1), w).astype(jnp.bfloat16)
-    wexp[...] = lax.dot_general(
-        w, chooser.astype(jnp.bfloat16), (((0,), (0,)), ((), ())), preferred_element_type=F32
-    )
+    w = jnp.where(swap, roll(w, 2 * LANES, 1), w)
+    tall = []
+    for m in range(4):
+        low, high = jnp.broadcast_to(w[2 * m:2 * m + 1], (8, 128)), jnp.broadcast_to(w[2 * m + 1:2 * m + 2], (8, 128))
+        tall.append(jnp.where(top, low, high))
+    wexp[...] = jnp.transpose(jnp.concatenate(tall * BLK, axis=0))
 
     def spread(c, carry):
         for slot in range(2):
@@ -507,8 +552,9 @@
         return carry
 
     lax.fori_loop(0, 24, from_columns, 0)
-    copies = send_x(1, corr) + send_t(1, corr) + send_z(1, corr)
-    local_part(corr, res, out_res, sign[3])
+    nothing = lambda: None
+    copies = send_all(1, corr, (nothing,) * 3)
+    local_part(corr, res, out_res, sign[3], (nothing,) * 2)
     far_part(1, out_res, copies, last, first)
 
 
@@ -588,10 +634,11 @@
         null_store.reshape(nulls),
         links,
     )
+    outs = [pltpu.with_memory_space_constraint(out, pltpu.VMEM) for out in outs]
     outs = pl.pallas_call(
         hand_over,
         out_shape=(jax.ShapeDtypeStruct(field, F32),) * 2,
-        in_specs=[pl.BlockSpec(memory_space=pl.ANY)] * 2,
+        in_specs=[vmem] * 2,
         out_specs=(hbm,) * 2,
         scratch_shapes=[pltpu.SemaphoreType.DMA((2,))],
         compiler_params=pltpu.CompilerParams(vmem_limit_bytes=66_200_000),

time: 56.6 us -> 29.9 us (0.53)
  Pallas kernels: 54.3 us -> 29.1 us
  local copies, waits for them, and re-layouts: 1.49 us -> 0 us
    pallas_call x1, Pallas kernels: 24.9 us -> 0.89 us  [per_device(): pl.pallas_call(hand_over, out_shape=(jax.ShapeDtypeStruct(field, F32),) *...]
    unnamed x4 -> x0, local copies, waits for them, and re-layouts: 1.49 us -> none
    pallas_call x1, Pallas kernels: 29.4 us -> 28.2 us  [per_device(): pl.pallas_call(functools.partial(kernel, counts), out_shape=(pltpu.VMEM(f...]
where the time goes in v2:
time: 29.9 us; the launch traced here: 29.8 us
  Pallas kernels  29.1 us (97%)
  between operations  0.64 us (2%)
    pallas_call x1, Pallas kernels, per_device(): pl.pallas_call(functools.partial(kernel, counts), out_shape=(pltpu.VMEM(f...  28.2 us
    pallas_call x1, Pallas kernels, per_device(): pl.pallas_call(hand_over, out_shape=(jax.ShapeDtypeStruct(field, F32),) *...  0.89 us

profile of v2, /device:TPU:0, one launch (start us, length us, event | category | flops | bytes accessed | tf_op | source)
XLA Modules:
  0.0 29.8 jit_solution(13042837992263527858)
XLA Ops:
  0.6 28.2 %shard_map.95 = (f32[768,128]{1,0:T(8,128)S(1)}, f32[768,128]{1,0:T(8,128)S(1)}) custom-call(s32[4]{0:T(128)} %bc_hbm.1, s32[2]{0:T(128)} %bitcast.19, f32[768,128]{1,0:T(8,128)} %bitcast.17, f32[768,128]{1,0:T(8,128)} %bitcast.18, f32[2304,128]{1,0:T(8,128)} %bitcast.16, f32[4608,128]{1,0:T(8,128)} %bitcast.15, bf16[2,2,24,12,16,128]{5,4,3,2,1,0:T(8,128)(2,1)} %bitcast.13, ...), custom_call_target="tpu_custom_call" | custom-call | tf_op jit(solution)/shard_map/pallas_call | solution.py:586
  28.9 0.9 %shard_map.96 = (f32[768,128]{1,0:T(8,128)}, f32[768,128]{1,0:T(8,128)}) custom-call(f32[768,128]{1,0:T(8,128)S(1)} %get-tuple-element.6.it_in, f32[768,128]{1,0:T(8,128)S(1)} %get-tuple-element.7.res_in), custom_call_target="tpu_custom_call" | custom-call | tf_op jit(solution)/shard_map/pallas_call | solution.py:638

commit v3 on v2

--- a/solution.py
+++ b/solution.py
@@ -119,6 +119,15 @@
 
 def wide(a, b):
     return a.astype(F32) * b.astype(F32)
+
+
+def several(count, step, work):
+    def body(g, carry):
+        for j in range(step):
+            work(g * step + j)
+        return carry
+
+    lax.fori_loop(0, count // step, body, 0)
 
 
 def kernel(
@@ -152,18 +161,16 @@
     load_z = load(3, link_part(ga_hbm, 1), link_part(ga, 1))
     load_bc = load(4, bc_hbm, bc_ref)
     load_slot = load(5, slot_hbm, slot_ref)
-    load_y = load(6, link_part(ga_hbm, 3), link_part(ga, 3))
-    load_src = load(7, src_hbm, src)
-    load_cl = load(8, cl_hbm, cl)
-    load_co = load(9, co_hbm, co)
-    load_nu = load(10, nu_hbm, nu)
-
-    def send(phase, number, source, target, device):
+
+    def message(phase, number, source, target, device):
         slot = (phase % 2) * 6 + number
-        copy = pltpu.make_async_remote_copy(
-            src_ref=source, dst_ref=target, send_sem=send_sem.at[slot], recv_sem=recv_sem.at[slot],
+        return pltpu.make_async_remote_copy(
+            src_ref=source, dst_ref=target, send_sem=send_sem.at[number], recv_sem=recv_sem.at[slot],
             device_id=device, device_id_type=MESH,
         )
+
+    def send(*parts):
+        copy = message(*parts)
         copy.start()
         return copy
 
@@ -192,19 +199,29 @@
             value = jnp.where(group == t, moved[t], value)
         return value
 
-    def pack_links(ri, carry):
-        for m in range(9):
-            base = (((4 + ri) * 9 + m) * T)
-            put_rows(gx, ri * 9 + m, gathered([rows(ga, base + t) for t in range(T)], LY))
-        return carry
-
-    def ordered(d, number, name, outgoing, incoming, choice):
-        copies = [None, None]
-        for turn in range(2):
-            way = choice if turn == 0 else 1 - choice
+    def pack_links():
+        for ri in range(2):
+            for m in range(9):
+                base = (((4 + ri) * 9 + m) * T)
+                put_rows(gx, ri * 9 + m, gathered([rows(ga, base + t) for t in range(T)], LY))
+
+    def halo(d, number, name, outgoing, incoming, choice):
+        copies = []
+        for way in (choice, 1 - choice):
             target = {name: lax.rem(place[name] + counts[name] - 1 + 2 * way, counts[name])}
-            copies[turn] = send(d * 4, number + way, outgoing.at[d, way], incoming.at[d, way], target)
+            copies.append(message(d * 4, number + way, outgoing.at[d, way], incoming.at[d, way], target))
         return copies
+
+    def halos(d):
+        return (
+            halo(d, 0, "xy", sx, rx, (place["xy"] + 1) // counts["xy"]),
+            halo(d, 2, "ta", st, rt, lax.rem(place["ta"], 2)),
+            halo(d, 4, "gz", sz, rz, 0),
+        )
+
+    def start_all(copies):
+        for copy in copies:
+            copy.start()
 
     def fill_x(d, field):
         sites = [site(field, t) for t in range(T)]
@@ -231,19 +248,7 @@
         half = link_dagger(gauge_edge_z, project(high, 1, False))
         put_half(half, lambda c, v: put_rows(sz.at[d, 1], c, v, T))
 
-    def send_all(d, field, before):
-        before[0]()
-        fill_t(d, field)
-        copies_t = ordered(d, 2, "ta", st, rt, lax.rem(place["ta"], 2))
-        before[1]()
-        fill_x(d, field)
-        copies_x = ordered(d, 0, "xy", sx, rx, (place["xy"] + 1) // counts["xy"])
-        before[2]()
-        fill_z(d, field)
-        copies_z = ordered(d, 4, "gz", sz, rz, 0)
-        return copies_x + copies_t + copies_z
-
-    def local_part(field, base, out, sign_y, before):
+    def local_part(field, base, out, sign_y, before, moved=None):
         def keep(total, t, old):
             for s in range(4):
                 for c in range(3):
@@ -310,6 +315,9 @@
                     here, there = k * T + t, (12 + k) * T + t
                     put_rows(out, here, rows(out, here) + rows(base, here) - re)
                     put_rows(out, there, rows(out, there) + rows(base, there) - im)
+                    if moved is not None:
+                        for at, value in ((here, psi[s][c][0]), (there, psi[s][c][1])):
+                            put_rows(moved, at, rows(itv, at) + value)
             return carry
 
         lax.fori_loop(0, T, on_site, 0)
@@ -321,9 +329,12 @@
                     spot = where(ri * 12 + s * 3 + c)
                     out[spot] = out[spot] + 0.5 * total[s][c][ri]
 
+    def wait_all(copies):
+        for copy in copies:
+            copy.wait()
+
     def far_part(d, out, copies, last, first):
-        copies[4].wait()
-        copies[5].wait()
+        wait_all(copies[2])
         edge = half_of(lambda c: rows(rz.at[d, 0], c, T) * last[1])
         total = zero_spinor(edge[0][0][0])
         rebuild(total, link_times(gauge_edge_z, edge), 1, True)
@@ -331,8 +342,7 @@
         total = zero_spinor(edge[0][0][0])
         rebuild(total, half_of(lambda c: rows(rz.at[d, 1], c, T) * first[1]), 1, False)
         add_to(out, total, lambda k: (pl.ds(k * T * 8, T, stride=8), slice(None)))
-        copies[2].wait()
-        copies[3].wait()
+        wait_all(copies[1])
         total = zero_spinor(lane.astype(F32))
         edge = half_of(lambda c: rows(rt.at[d, 0], c) * last[0])
         rebuild(total, link_times(gauge(0, T - 1), edge), 0, True)
@@ -340,8 +350,7 @@
         total = zero_spinor(lane.astype(F32))
         rebuild(total, half_of(lambda c: rows(rt.at[d, 1], c) * first[0]), 0, False)
         add_to(out, total, lambda k: (pl.ds(k * T * 8, 8), slice(None)))
-        copies[1].wait()
-        copies[0].wait()
+        wait_all(copies[0])
         edge = half_of(lambda c: rows(rx.at[d, 0], c) * last[2])
         put_half(link_times(gauge_edge_x, edge), lambda c, v: put_rows(hx, c, v))
         way = jnp.where(group == T - 1, -1.0, 1.0)
@@ -361,18 +370,26 @@
                     total[2 + s][c] = add_turned(total[2 + s][c], (z[0] * way, z[1] * way), power)
             add_to(out, total, lambda k: (pl.ds((k * T + t) * 8, 8), slice(None)))
 
-    def ready_t():
-        load_it.wait()
-        load_t.wait()
-        pl.semaphore_wait(barrier, 6)
-
-    def ready_x():
-        load_x.wait()
-        lax.fori_loop(0, 2, pack_links, 0)
-
-    copies = send_all(0, itv, (ready_t, ready_x, load_z.wait))
+    load_it.wait()
+    load_cl = load(0, cl_hbm, cl)
+    load_x.wait()
+    load_y = load(1, link_part(ga_hbm, 3), link_part(ga, 3))
+    pack_links()
+    fill_x(0, itv)
+    load_t.wait()
+    load_src = load(2, src_hbm, src)
+    fill_t(0, itv)
+    load_z.wait()
+    load_nu = load(3, nu_hbm, nu)
+    fill_z(0, itv)
     load_bc.wait()
+    load_co = load(4, co_hbm, co)
     load_slot.wait()
+    red[...] = jnp.zeros(red.shape, F32)
+    pl.semaphore_wait(barrier, 6)
+    copies = halos(0)
+    for group_of in copies:
+        start_all(group_of)
     sign = [bc_ref[mu].astype(F32) for mu in range(4)]
     last = [jnp.where(place[n] == counts[n] - 1, sign[i], 1.0) for i, n in enumerate(names)]
     first = [jnp.where(place[n] == 0, sign[i], 1.0) for i, n in enumerate(names)]
@@ -396,7 +413,7 @@
 
     far_part(0, res, copies, last, first)
 
-    def to_columns(k, carry):
+    def to_columns(k):
         low, high = [], []
         for pair, group_of in enumerate((low, high)):
             a, b = rows(res, k * T + 2 * pair), rows(res, k * T + 2 * pair + 1)
@@ -407,13 +424,11 @@
             value = jnp.concatenate([low[slot], high[slot]], axis=0).astype(jnp.bfloat16)
             fc[slot, k] = value
             fc[slot, 24 + k] = -value
-        return carry
-
-    lax.fori_loop(0, 24, to_columns, 0)
+
+    several(24, 4, to_columns)
     load_nu.wait()
-    red[...] = jnp.zeros(red.shape, F32)
     for slot in range(2):
-        def restrict(g, carry):
+        def restrict(g):
             sums = [None] * 4
             for s in range(12):
                 fr, fi, minus = fc[slot, s], fc[slot, 12 + s], fc[slot, 24 + s]
@@ -428,9 +443,8 @@
                 for ri in range(2):
                     value = sums[2 * j + ri]
                     put_rows(red, (2 * slot + ri) * LANES + g * 2 + j, value[:8] + value[8:])
-            return carry
-
-        lax.fori_loop(0, nv // 2, restrict, 0)
+
+        several(nv // 2, 4, restrict)
     gathered_rows = red[pl.ds(0, 128, stride=8), :]
     for r in range(1, 8):
         gathered_rows = gathered_rows + red[pl.ds(r, 128, stride=8), :]
@@ -514,14 +528,13 @@
         tall.append(jnp.where(top, low, high))
     wexp[...] = jnp.transpose(jnp.concatenate(tall * BLK, axis=0))
 
-    def spread(c, carry):
+    def spread(c):
         for slot in range(2):
             values = [wexp[pl.ds((2 * slot + ri) * LANES + c, 1), :] for ri in range(2)]
             for at, v in enumerate((values[0], values[1], -values[1])):
                 wv[slot, at, c] = jnp.broadcast_to(v, (2 * 8, 128)).astype(jnp.bfloat16)
-        return carry
-
-    lax.fori_loop(0, nv, spread, 0)
+
+    several(nv, 4, spread)
     for slot in range(2):
         def prolong(q, carry):
             sums = [None] * 4
@@ -541,20 +554,24 @@
 
         lax.fori_loop(0, 6, prolong, 0)
 
-    def from_columns(k, carry):
+    def from_columns(k):
         for pair in range(2):
             part_0, part_1 = pc[0, k, pl.ds(8 * pair, 8), :], pc[1, k, pl.ds(8 * pair, 8), :]
             part_0, part_1 = jnp.where(swap, part_1, part_0), jnp.where(swap, part_0, part_1)
             for h, value in enumerate(split_columns(part_0, part_1, top)):
                 at = k * T + 2 * pair + h
                 put_rows(corr, at, value)
-                put_rows(out_it, at, rows(itv, at) + value)
-        return carry
-
-    lax.fori_loop(0, 24, from_columns, 0)
+
+    several(24, 4, from_columns)
     nothing = lambda: None
-    copies = send_all(1, corr, (nothing,) * 3)
-    local_part(corr, res, out_res, sign[3], (nothing,) * 2)
+    copies = halos(1)
+    fill_x(1, corr)
+    start_all(copies[0])
+    fill_t(1, corr)
+    start_all(copies[1])
+    fill_z(1, corr)
+    start_all(copies[2])
+    local_part(corr, res, out_res, sign[3], (nothing,) * 2, out_it)
     far_part(1, out_res, copies, last, first)
 
 
@@ -617,8 +634,8 @@
             pltpu.VMEM((128, 128), F32),
             pltpu.VMEM((columns, 3, nv, BLK * BLK, 128), jnp.bfloat16),
             pltpu.VMEM((columns, 24, BLK * BLK, 128), F32),
-            pltpu.SemaphoreType.DMA((11,)),
-            pltpu.SemaphoreType.DMA((12,)),
+            pltpu.SemaphoreType.DMA((6,)),
+            pltpu.SemaphoreType.DMA((6,)),
             pltpu.SemaphoreType.DMA((12,)),
         ],
         compiler_params=pltpu.CompilerParams(

time: 29.9 us -> 29 us (0.970)
  Pallas kernels: 29.1 us -> 28.2 us
    pallas_call x1, Pallas kernels: 28.2 us -> 27.4 us  [per_device(): pl.pallas_call(functools.partial(kernel, counts), out_shape=(pltpu.VMEM(f...]
where the time goes in v3:
time: 29 us; the launch traced here: 28.9 us
  Pallas kernels  28.2 us (97%)
  between operations  0.64 us (2%)
    pallas_call x1, Pallas kernels, per_device(): pl.pallas_call(functools.partial(kernel, counts), out_shape=(pltpu.VMEM(f...  27.4 us
    pallas_call x1, Pallas kernels, per_device(): pl.pallas_call(hand_over, out_shape=(jax.ShapeDtypeStruct(field, F32),) *...  0.89 us

profile of v3, /device:TPU:0, one launch (start us, length us, event | category | flops | bytes accessed | tf_op | source)
XLA Modules:
  0.0 28.9 jit_solution(11851100331191017298)
XLA Ops:
  0.6 27.4 %shard_map.95 = (f32[768,128]{1,0:T(8,128)S(1)}, f32[768,128]{1,0:T(8,128)S(1)}) custom-call(s32[4]{0:T(128)} %bc_hbm.1, s32[2]{0:T(128)} %bitcast.19, f32[768,128]{1,0:T(8,128)} %bitcast.17, f32[768,128]{1,0:T(8,128)} %bitcast.18, f32[2304,128]{1,0:T(8,128)} %bitcast.16, f32[4608,128]{1,0:T(8,128)} %bitcast.15, bf16[2,2,24,12,16,128]{5,4,3,2,1,0:T(8,128)(2,1)} %bitcast.13, ...), custom_call_target="tpu_custom_call" | custom-call | tf_op jit(solution)/shard_map/pallas_call | solution.py:603
  28.0 0.9 %shard_map.96 = (f32[768,128]{1,0:T(8,128)}, f32[768,128]{1,0:T(8,128)}) custom-call(f32[768,128]{1,0:T(8,128)S(1)} %get-tuple-element.6.it_in, f32[768,128]{1,0:T(8,128)S(1)} %get-tuple-element.7.res_in), custom_call_target="tpu_custom_call" | custom-call | tf_op jit(solution)/shard_map/pallas_call | solution.py:655

commit v4 on v3

--- a/solution.py
+++ b/solution.py
@@ -9,7 +9,6 @@
 
 BLK = 4
 LY = 32
-CITERS = 4
 MASS_TERM = 3.8
 RELAX_WEIGHT = 0.4
 MESH = pl.DeviceIdType.MESH
@@ -132,8 +131,8 @@
 
 def kernel(
     counts, bc_hbm, slot_hbm, src_hbm, it_hbm, ga_hbm, cl_hbm, nu_hbm, co_hbm, out_it, out_res,
-    bc_ref, slot_ref, src, itv, ga, cl, nu, co, res, corr, gx, st, sx, sz, rt, rx, rz, hx, fc, red, pk, part, wbuf,
-    wr, rhs, wexp, wv, pc, load_sem, send_sem, recv_sem,
+    bc_ref, slot_ref, src, itv, ga, cl, nu, co, res, corr, gx, st, sx, sz, rt, rx, rz, hx, fc, red, pk, pks, part, wone,
+    rh, wr0, wr1, wr2, wmid, fin, zr, zfin, wexp, wv, pc, load_sem, send_sem, recv_sem,
 ):
     T = BLK
     names = ("ta", "gz", "xy")
@@ -151,28 +150,38 @@
     load_it = load(0, it_hbm, itv)
     load_x = load(1, link_part(ga_hbm, 2), link_part(ga, 2))
     place = {n: lax.axis_index(n) for n in names}
-    ahead = {n: {n: lax.rem(place[n] + 1, counts[n])} for n in names}
-    behind = {n: {n: lax.rem(place[n] + counts[n] - 1, counts[n])} for n in names}
+    depth = counts["gz"]
+    core = lax.rem(place["gz"], 2)
+    several_pairs = depth > 2
+
+    def along_z(step):
+        return {"gz": lax.rem(place["gz"] + depth + step, depth)}
+
+    def pair_of(other):
+        return {"gz": place["gz"] - core + other}
+
+    def away(name, step, other):
+        return {name: lax.rem(place[name] + counts[name] + step, counts[name]), **pair_of(other)}
+
+    ways = (("xy", -1), ("xy", 1), ("ta", -1), ("ta", 1))
+    greeted = [away(name, step, other) for name, step in ways for other in range(2)]
+    greeted += [along_z(step) for step in ((-1, 1, -2, 2) if several_pairs else (1,))]
     barrier = pltpu.get_barrier_semaphore()
-    for n in ("xy", "ta", "gz"):
-        for target in (ahead[n], behind[n]):
-            pl.semaphore_signal(barrier, inc=1, device_id=target, device_id_type=MESH)
+    for target in greeted:
+        pl.semaphore_signal(barrier, inc=1, device_id=target, device_id_type=MESH)
     load_t = load(2, link_part(ga_hbm, 0), link_part(ga, 0))
     load_z = load(3, link_part(ga_hbm, 1), link_part(ga, 1))
     load_bc = load(4, bc_hbm, bc_ref)
     load_slot = load(5, slot_hbm, slot_ref)
 
-    def message(phase, number, source, target, device):
-        slot = (phase % 2) * 6 + number
+    def message(sent, arrived, source, target, device):
         return pltpu.make_async_remote_copy(
-            src_ref=source, dst_ref=target, send_sem=send_sem.at[number], recv_sem=recv_sem.at[slot],
+            src_ref=source, dst_ref=target, send_sem=send_sem.at[sent], recv_sem=recv_sem.at[arrived],
             device_id=device, device_id_type=MESH,
         )
 
-    def send(*parts):
-        copy = message(*parts)
-        copy.start()
-        return copy
+    def await_bytes(sem, shaped):
+        pltpu.make_async_copy(shaped, shaped, sem).wait()
 
     row = lax.broadcasted_iota(jnp.int32, (8, 128), 0)
     lane = lax.broadcasted_iota(jnp.int32, (8, 128), 1)
@@ -209,7 +218,7 @@
         copies = []
         for way in (choice, 1 - choice):
             target = {name: lax.rem(place[name] + counts[name] - 1 + 2 * way, counts[name])}
-            copies.append(message(d * 4, number + way, outgoing.at[d, way], incoming.at[d, way], target))
+            copies.append(message(number + way, number + way, outgoing.at[d, way], incoming.at[d, way], target))
         return copies
 
     def halos(d):
@@ -380,13 +389,13 @@
     load_src = load(2, src_hbm, src)
     fill_t(0, itv)
     load_z.wait()
-    load_nu = load(3, nu_hbm, nu)
+    load_co = load(3, co_hbm, co)
     fill_z(0, itv)
     load_bc.wait()
-    load_co = load(4, co_hbm, co)
+    load_nu = load(4, nu_hbm, nu)
     load_slot.wait()
     red[...] = jnp.zeros(red.shape, F32)
-    pl.semaphore_wait(barrier, 6)
+    pl.semaphore_wait(barrier, len(greeted))
     copies = halos(0)
     for group_of in copies:
         start_all(group_of)
@@ -410,6 +419,13 @@
                 value = value + roll(parts[g], LANES * g, 1)
             pk[k, i] = value
         return carry
+
+    load_co.wait()
+    lax.fori_loop(0, 9, pack_coarse, 0)
+
+    @pl.when(core == 0)
+    def _():
+        message(6, 8, pk, pks, pair_of(1)).start()
 
     far_part(0, res, copies, last, first)
 
@@ -460,67 +476,122 @@
         here = jnp.where(row == 2 * m, lower, upper)
         value = here if m == 0 else jnp.where(row // 2 == m, here, value)
     value = jnp.where(swap, roll(value, 2 * LANES, 1), value)
-    rhs[...] = value
-    wbuf[0] = RELAX_WEIGHT * value
+    rh[1] = value
+    wone[...] = RELAX_WEIGHT * value
+    for d, (name, step) in enumerate(ways):
+        message(0, 6, wone, wr0.at[core, d], away(name, step, 1)).start()
+    if several_pairs:
+        message(7, 10, wone, zr.at[0, 1 - core], along_z(3 * core - 1)).start()
 
     even = (group & 1) == 0
     turn = jnp.where(even, 1.0, -1.0)
+    half = 2 * LANES
+    block = 8
 
     def pairs_of(w):
         return w * turn, jnp.where(even, roll(w, -LANES, 1), roll(w, LANES, 1))
 
-    def products(vectors, i, sums):
+    def products(table, vectors, i, sums):
         for k, (wa, wb) in vectors:
-            y = pk[k, i]
+            y = table[k, i]
             sums = (y * wa, y * wb) if sums is None else (sums[0] + y * wa, sums[1] + y * wb)
         return sums
 
-    block = 8
-    for it in range(CITERS - 1):
-        phase = it + 1
-        own = wbuf[it]
-        targets = [behind["xy"], ahead["xy"], behind["ta"], ahead["ta"], behind["gz"], ahead["gz"]]
-        copies = [send(phase, d, wbuf.at[it], wr.at[it, d], targets[d]) for d in range(6)]
-        if it == 0:
-            load_co.wait()
-            lax.fori_loop(0, 9, pack_coarse, 0)
-        vectors = [(0, pairs_of(own)), (7, pairs_of(roll(own, -1, 0))), (8, pairs_of(roll(own, 1, 0)))]
-
-        def near(g, carry):
+    def near(table, own, above, below, h):
+        turned = roll(own, half, 1)
+        next_z = jnp.where(lane < half, turned, roll(above, half, 1))
+        last_z = jnp.where(lane < half, roll(below, half, 1), turned)
+        places = ((0, own), (7, roll(own, -1, 0)), (8, roll(own, 1, 0)), (3, next_z), (4, last_z))
+        vectors = [(k, pairs_of(w)) for k, w in places]
+
+        def body(g, carry):
             for j in range(block):
                 i = g * block + j
-                part[0, i], part[1, i] = products(vectors, i, None)
+                part[h, 0, i], part[h, 1, i] = products(table, vectors, i, None)
             return carry
 
-        lax.fori_loop(0, nv // block, near, 0)
-        copies[4].wait()
-        copies[5].wait()
-        half = 2 * LANES
-        next_z = jnp.where(lane < half, roll(own, half, 1), roll(wr[it, 4], half, 1))
-        last_z = jnp.where(lane < half, roll(wr[it, 5], half, 1), roll(own, half, 1))
-        z_vectors = [(3, pairs_of(next_z)), (4, pairs_of(last_z))]
-
-        def middle(g, carry):
-            for j in range(block):
-                i = g * block + j
-                part[0, i], part[1, i] = products(z_vectors, i, (part[0, i], part[1, i]))
-            return carry
-
-        lax.fori_loop(0, nv // block, middle, 0)
-        for d in range(4):
-            copies[d].wait()
-        far_vectors = [(k, pairs_of(wr[it, d])) for k, d in ((1, 2), (2, 3), (5, 0), (6, 1))]
+        lax.fori_loop(0, nv // block, body, 0)
+
+    def far(table, arrived, own, known, h):
+        vectors = [(k, pairs_of(arrived[d])) for k, d in ((1, 2), (2, 3), (5, 0), (6, 1))]
         applied = jnp.zeros((8, 128), F32)
         for i in range(nv):
-            sums = products(far_vectors, i, (part[0, i], part[1, i]))
+            sums = products(table, vectors, i, (part[h, 0, i], part[h, 1, i]))
             for ri in range(2):
                 for col in range(2):
                     mine = (lane < half) if col == 0 else (lane >= half)
                     whole = jnp.sum(jnp.where(mine, sums[ri], 0.0), axis=1, keepdims=True)
                     applied = jnp.where(lane == LANES * (2 * col + ri) + i, whole, applied)
-        wbuf[it + 1] = own + RELAX_WEIGHT * (rhs[...] - (2.0 * own + applied))
-
-    w = wbuf[CITERS - 1]
+        return own + RELAX_WEIGHT * (known - (2.0 * own + applied))
+
+    @pl.when(core == 0)
+    def _():
+        message(0, 7, rh.at[1], rh.at[0], pair_of(1)).start()
+
+    @pl.when(core == 1)
+    def _():
+        tables = (pks, pk)
+        await_bytes(recv_sem.at[7], rh.at[0])
+        wmid[0, 0] = RELAX_WEIGHT * rh[0]
+        wmid[0, 1] = wone[...]
+        await_bytes(recv_sem.at[8], pks)
+        for it in range(2):
+            if it == 1:
+                for d, (name, step) in enumerate(ways):
+                    message(0, 9, wmid.at[1], wr1.at[d], away(name, step, 1)).start()
+                if several_pairs:
+                    message(7, 11, wmid.at[1, 0], zr.at[1, 1], along_z(-2)).start()
+                    message(7, 11, wmid.at[1, 1], zr.at[1, 0], along_z(2)).start()
+            lower, upper = wmid[it, 0], wmid[it, 1]
+            below, above = upper, lower
+            if several_pairs:
+                await_bytes(recv_sem.at[10 + it], zr.at[it])
+                below, above = zr[it, 0], zr[it, 1]
+            near(tables[0], lower, upper, below, 0)
+            near(tables[1], upper, above, lower, 1)
+            if it == 0:
+                await_bytes(recv_sem.at[6], wr0)
+            else:
+                await_bytes(recv_sem.at[9], wr1)
+            for h in range(2):
+                arrived = [wr0[h, d] if it == 0 else wr1[d, h] for d in range(4)]
+                wmid[it + 1, h] = far(tables[h], arrived, wmid[it, h], rh[h], h)
+        for d, (name, step) in enumerate(ways):
+            message(0, 6, wmid.at[2, 0], wr2.at[d], away(name, step, 0)).start()
+        message(0, 7, wmid.at[2], fin, pair_of(0)).start()
+        for d, (name, step) in enumerate(ways):
+            message(0, 6, wmid.at[2, 1], wr2.at[d], away(name, step, 1)).start()
+        if several_pairs:
+            message(7, 12, wmid.at[2, 1], zfin, along_z(1)).start()
+            message(7, 12, wmid.at[2, 0], zfin, along_z(-2)).start()
+        fin[0] = wmid[2, 1]
+        fin[1] = wmid[2, 0]
+
+    @pl.when(core == 0)
+    def _():
+        await_bytes(recv_sem.at[7], fin)
+
+    own, above, below = fin[0], fin[1], fin[1]
+    if several_pairs:
+        await_bytes(recv_sem.at[12], zfin)
+        above, below = jnp.where(core == 0, above, zfin[...]), jnp.where(core == 0, zfin[...], below)
+    near(pk, own, above, below, 0)
+    await_bytes(recv_sem.at[6], wr2)
+    w = far(pk, [wr2[d] for d in range(4)], own, rh[1], 0)
+
+    @pl.when(core == 0)
+    def _():
+        await_bytes(send_sem.at[0], pk.at[0, pl.ds(0, 5)])
+        await_bytes(send_sem.at[6], pk)
+        if several_pairs:
+            await_bytes(send_sem.at[7], wone)
+
+    @pl.when(core == 1)
+    def _():
+        await_bytes(send_sem.at[0], pk.at[0, pl.ds(0, 22)])
+        if several_pairs:
+            await_bytes(send_sem.at[7], pk.at[0, pl.ds(0, 5)])
+
     w = jnp.where(swap, roll(w, 2 * LANES, 1), w)
     tall = []
     for m in range(4):
@@ -627,16 +698,23 @@
             pltpu.VMEM((columns, 48, BLK * BLK, 128), jnp.bfloat16),
             pltpu.VMEM((128 * 8, 128), F32),
             pltpu.VMEM((9, nv) + tile, F32),
-            pltpu.VMEM((2, nv) + tile, F32),
-            pltpu.VMEM((CITERS,) + tile, F32),
-            pltpu.VMEM((CITERS - 1, 6) + tile, F32),
+            pltpu.VMEM((9, nv) + tile, F32),
+            pltpu.VMEM((2, 2, nv) + tile, F32),
+            pltpu.VMEM(tile, F32),
+            pltpu.VMEM((2,) + tile, F32),
+            pltpu.VMEM((2, 4) + tile, F32),
+            pltpu.VMEM((4, 2) + tile, F32),
+            pltpu.VMEM((4,) + tile, F32),
+            pltpu.VMEM((3, 2) + tile, F32),
+            pltpu.VMEM((2,) + tile, F32),
+            pltpu.VMEM((2, 2) + tile, F32),
             pltpu.VMEM(tile, F32),
             pltpu.VMEM((128, 128), F32),
             pltpu.VMEM((columns, 3, nv, BLK * BLK, 128), jnp.bfloat16),
             pltpu.VMEM((columns, 24, BLK * BLK, 128), F32),
             pltpu.SemaphoreType.DMA((6,)),
-            pltpu.SemaphoreType.DMA((6,)),
-            pltpu.SemaphoreType.DMA((12,)),
+            pltpu.SemaphoreType.DMA((8 if counts["gz"] > 2 else 7,)),
+            pltpu.SemaphoreType.DMA((13 if counts["gz"] > 2 else 10,)),
         ],
         compiler_params=pltpu.CompilerParams(
             collective_id=0, has_side_effects=True, vmem_limit_bytes=66_200_000

time: 29 us -> 28.6 us (0.986)
  Pallas kernels: 28.2 us -> 27.8 us
    pallas_call x1, Pallas kernels: 27.4 us -> 26.9 us  [per_device(): pl.pallas_call(functools.partial(kernel, counts), out_shape=(pltpu.VMEM(f...]
where the time goes in v4:
time: 28.6 us; the launch traced here: 28.4 us
  Pallas kernels  27.8 us (97%)
  between operations  0.64 us (2%)
    pallas_call x1, Pallas kernels, per_device(): pl.pallas_call(functools.partial(kernel, counts), out_shape=(pltpu.VMEM(f...  26.9 us
    pallas_call x1, Pallas kernels, per_device(): pl.pallas_call(hand_over, out_shape=(jax.ShapeDtypeStruct(field, F32),) *...  0.89 us

profile of v4, /device:TPU:0, one launch (start us, length us, event | category | flops | bytes accessed | tf_op | source)
XLA Modules:
  0.0 28.4 jit_solution(7509186041027367595)
XLA Ops:
  0.6 26.9 %shard_map.95 = (f32[768,128]{1,0:T(8,128)S(1)}, f32[768,128]{1,0:T(8,128)S(1)}) custom-call(s32[4]{0:T(128)} %bc_hbm.1, s32[2]{0:T(128)} %bitcast.19, f32[768,128]{1,0:T(8,128)} %bitcast.17, f32[768,128]{1,0:T(8,128)} %bitcast.18, f32[2304,128]{1,0:T(8,128)} %bitcast.16, f32[4608,128]{1,0:T(8,128)} %bitcast.15, bf16[2,2,24,12,16,128]{5,4,3,2,1,0:T(8,128)(2,1)} %bitcast.13, ...), custom_call_target="tpu_custom_call" | custom-call | tf_op jit(solution)/shard_map/pallas_call | solution.py:674
  27.5 0.9 %shard_map.96 = (f32[768,128]{1,0:T(8,128)}, f32[768,128]{1,0:T(8,128)}) custom-call(f32[768,128]{1,0:T(8,128)S(1)} %get-tuple-element.6.it_in, f32[768,128]{1,0:T(8,128)S(1)} %get-tuple-element.7.res_in), custom_call_target="tpu_custom_call" | custom-call | tf_op jit(solution)/shard_map/pallas_call | solution.py:733

commit v5 on v4

--- a/solution.py
+++ b/solution.py
@@ -222,15 +222,21 @@
         return copies
 
     def halos(d):
+        to_first = {n: (place[n] + 1) // counts[n] for n in ("xy", "ta")}
         return (
-            halo(d, 0, "xy", sx, rx, (place["xy"] + 1) // counts["xy"]),
-            halo(d, 2, "ta", st, rt, lax.rem(place["ta"], 2)),
+            halo(d, 0, "xy", sx, rx, to_first["xy"]),
+            halo(d, 2, "ta", st, rt, lax.rem(place["ta"], 2) if d == 0 else to_first["ta"]),
             halo(d, 4, "gz", sz, rz, 0),
         )
 
     def start_all(copies):
         for copy in copies:
             copy.start()
+
+    def start_if(which, copies):
+        @pl.when(core == which)
+        def _():
+            start_all(copies)
 
     def fill_x(d, field):
         sites = [site(field, t) for t in range(T)]
@@ -257,7 +263,7 @@
         half = link_dagger(gauge_edge_z, project(high, 1, False))
         put_half(half, lambda c, v: put_rows(sz.at[d, 1], c, v, T))
 
-    def local_part(field, base, out, sign_y, before, moved=None):
+    def local_part(field, base, out, sign_y, before, later, moved=None):
         def keep(total, t, old):
             for s in range(4):
                 for c in range(3):
@@ -307,6 +313,7 @@
 
         lax.fori_loop(0, T, along_t_y, 0)
         before[1]()
+        later()
 
         def on_site(t, carry):
             psi = site(field, t)
@@ -408,7 +415,8 @@
         load_src.wait()
         load_cl.wait()
 
-    local_part(itv, src, res, sign[3], (load_y.wait, ready_site))
+    nothing = lambda: None
+    local_part(itv, src, res, sign[3], (load_y.wait, ready_site), nothing)
 
     def pack_coarse(k, carry):
         for i in range(nv):
@@ -479,9 +487,9 @@
     rh[1] = value
     wone[...] = RELAX_WEIGHT * value
     for d, (name, step) in enumerate(ways):
-        message(0, 6, wone, wr0.at[core, d], away(name, step, 1)).start()
+        message(0, 6 + 4 * core, wone, wr0.at[core, d], away(name, step, 1)).start()
     if several_pairs:
-        message(7, 10, wone, zr.at[0, 1 - core], along_z(3 * core - 1)).start()
+        message(7, 13, wone, zr.at[0, 1 - core], along_z(3 * core - 1)).start()
 
     even = (group & 1) == 0
     turn = jnp.where(even, 1.0, -1.0)
@@ -536,34 +544,29 @@
         wmid[0, 1] = wone[...]
         await_bytes(recv_sem.at[8], pks)
         for it in range(2):
-            if it == 1:
-                for d, (name, step) in enumerate(ways):
-                    message(0, 9, wmid.at[1], wr1.at[d], away(name, step, 1)).start()
-                if several_pairs:
-                    message(7, 11, wmid.at[1, 0], zr.at[1, 1], along_z(-2)).start()
-                    message(7, 11, wmid.at[1, 1], zr.at[1, 0], along_z(2)).start()
             lower, upper = wmid[it, 0], wmid[it, 1]
             below, above = upper, lower
             if several_pairs:
-                await_bytes(recv_sem.at[10 + it], zr.at[it])
+                await_bytes(recv_sem.at[13 + it], zr.at[it])
                 below, above = zr[it, 0], zr[it, 1]
+            near(tables[1], upper, above, lower, 1)
             near(tables[0], lower, upper, below, 0)
-            near(tables[1], upper, above, lower, 1)
-            if it == 0:
-                await_bytes(recv_sem.at[6], wr0)
-            else:
-                await_bytes(recv_sem.at[9], wr1)
-            for h in range(2):
-                arrived = [wr0[h, d] if it == 0 else wr1[d, h] for d in range(4)]
-                wmid[it + 1, h] = far(tables[h], arrived, wmid[it, h], rh[h], h)
-        for d, (name, step) in enumerate(ways):
-            message(0, 6, wmid.at[2, 0], wr2.at[d], away(name, step, 0)).start()
+            for h in (1, 0):
+                source = wr0 if it == 0 else wr1
+                await_bytes(recv_sem.at[(6, 10)[h] if it == 0 else (9, 11)[h]], source.at[h])
+                wmid[it + 1, h] = far(tables[h], [source[h, d] for d in range(4)], wmid[it, h], rh[h], h)
+                done = wmid.at[it + 1, h]
+                for d, (name, step) in enumerate(ways):
+                    if it == 0:
+                        message(0, (9, 11)[h], done, wr1.at[h, d], away(name, step, 1)).start()
+                    else:
+                        message(0, 12, done, wr2.at[d], away(name, step, h)).start()
+                if several_pairs:
+                    if it == 0:
+                        message(7, 14, done, zr.at[1, 1 - h], along_z(4 * h - 2)).start()
+                    else:
+                        message(7, 15, done, zfin, along_z(3 * h - 2)).start()
         message(0, 7, wmid.at[2], fin, pair_of(0)).start()
-        for d, (name, step) in enumerate(ways):
-            message(0, 6, wmid.at[2, 1], wr2.at[d], away(name, step, 1)).start()
-        if several_pairs:
-            message(7, 12, wmid.at[2, 1], zfin, along_z(1)).start()
-            message(7, 12, wmid.at[2, 0], zfin, along_z(-2)).start()
         fin[0] = wmid[2, 1]
         fin[1] = wmid[2, 0]
 
@@ -573,10 +576,10 @@
 
     own, above, below = fin[0], fin[1], fin[1]
     if several_pairs:
-        await_bytes(recv_sem.at[12], zfin)
+        await_bytes(recv_sem.at[15], zfin)
         above, below = jnp.where(core == 0, above, zfin[...]), jnp.where(core == 0, zfin[...], below)
     near(pk, own, above, below, 0)
-    await_bytes(recv_sem.at[6], wr2)
+    await_bytes(recv_sem.at[12], wr2)
     w = far(pk, [wr2[d] for d in range(4)], own, rh[1], 0)
 
     @pl.when(core == 0)
@@ -634,15 +637,14 @@
                 put_rows(corr, at, value)
 
     several(24, 4, from_columns)
-    nothing = lambda: None
     copies = halos(1)
     fill_x(1, corr)
-    start_all(copies[0])
+    start_if(0, copies[0])
     fill_t(1, corr)
-    start_all(copies[1])
+    start_if(0, copies[1])
     fill_z(1, corr)
     start_all(copies[2])
-    local_part(corr, res, out_res, sign[3], (nothing,) * 2, out_it)
+    local_part(corr, res, out_res, sign[3], (nothing,) * 2, lambda: start_if(1, copies[0] + copies[1]), out_it)
     far_part(1, out_res, copies, last, first)
 
 
@@ -703,7 +705,7 @@
             pltpu.VMEM(tile, F32),
             pltpu.VMEM((2,) + tile, F32),
             pltpu.VMEM((2, 4) + tile, F32),
-            pltpu.VMEM((4, 2) + tile, F32),
+            pltpu.VMEM((2, 4) + tile, F32),
             pltpu.VMEM((4,) + tile, F32),
             pltpu.VMEM((3, 2) + tile, F32),
             pltpu.VMEM((2,) + tile, F32),
@@ -714,7 +716,7 @@
             pltpu.VMEM((columns, 24, BLK * BLK, 128), F32),
             pltpu.SemaphoreType.DMA((6,)),
             pltpu.SemaphoreType.DMA((8 if counts["gz"] > 2 else 7,)),
-            pltpu.SemaphoreType.DMA((13 if counts["gz"] > 2 else 10,)),
+            pltpu.SemaphoreType.DMA((16 if counts["gz"] > 2 else 13,)),
         ],
         compiler_params=pltpu.CompilerParams(
             collective_id=0, has_side_effects=True, vmem_limit_bytes=66_200_000

time: 28.6 us -> 27.8 us (0.972)
  Pallas kernels: 27.8 us -> 27 us
    pallas_call x1, Pallas kernels: 26.9 us -> 26.1 us  [per_device(): pl.pallas_call(functools.partial(kernel, counts), out_shape=(pltpu.VMEM(f...]
where the time goes in v5:
time: 27.8 us; the launch traced here: 27.7 us
  Pallas kernels  27 us (97%)
  between operations  0.64 us (2%)
    pallas_call x1, Pallas kernels, per_device(): pl.pallas_call(functools.partial(kernel, counts), out_shape=(pltpu.VMEM(f...  26.1 us
    pallas_call x1, Pallas kernels, per_device(): pl.pallas_call(hand_over, out_shape=(jax.ShapeDtypeStruct(field, F32),) *...  0.89 us

profile of v5, /device:TPU:0, one launch (start us, length us, event | category | flops | bytes accessed | tf_op | source)
XLA Modules:
  0.0 27.7 jit_solution(12480285232881212703)
XLA Ops:
  0.6 26.1 %shard_map.95 = (f32[768,128]{1,0:T(8,128)S(1)}, f32[768,128]{1,0:T(8,128)S(1)}) custom-call(s32[4]{0:T(128)} %bc_hbm.1, s32[2]{0:T(128)} %bitcast.19, f32[768,128]{1,0:T(8,128)} %bitcast.17, f32[768,128]{1,0:T(8,128)} %bitcast.18, f32[2304,128]{1,0:T(8,128)} %bitcast.16, f32[4608,128]{1,0:T(8,128)} %bitcast.15, bf16[2,2,24,12,16,128]{5,4,3,2,1,0:T(8,128)(2,1)} %bitcast.13, ...), custom_call_target="tpu_custom_call" | custom-call | tf_op jit(solution)/shard_map/pallas_call | solution.py:676
  26.8 0.9 %shard_map.96 = (f32[768,128]{1,0:T(8,128)}, f32[768,128]{1,0:T(8,128)}) custom-call(f32[768,128]{1,0:T(8,128)S(1)} %get-tuple-element.6.it_in, f32[768,128]{1,0:T(8,128)S(1)} %get-tuple-element.7.res_in), custom_call_target="tpu_custom_call" | custom-call | tf_op jit(solution)/shard_map/pallas_call | solution.py:735

commit v6 on v5

--- a/solution.py
+++ b/solution.py
@@ -610,7 +610,7 @@
 
     several(nv, 4, spread)
     for slot in range(2):
-        def prolong(q, carry):
+        def prolong(q):
             sums = [None] * 4
             for c in range(nv):
                 vr, vi, minus = wv[slot, 0, c], wv[slot, 1, c], wv[slot, 2, c]
@@ -624,9 +624,8 @@
             for j in range(2):
                 for ri in range(2):
                     pc[slot, ri * 12 + q * 2 + j] = sums[2 * j + ri]
-            return carry
-
-        lax.fori_loop(0, 6, prolong, 0)
+
+        several(6, 2, prolong)
 
     def from_columns(k):
         for pair in range(2):
@@ -638,10 +637,10 @@
 
     several(24, 4, from_columns)
     copies = halos(1)
+    fill_t(1, corr)
+    start_if(0, copies[1])
     fill_x(1, corr)
     start_if(0, copies[0])
-    fill_t(1, corr)
-    start_if(0, copies[1])
     fill_z(1, corr)
     start_all(copies[2])
     local_part(corr, res, out_res, sign[3], (nothing,) * 2, lambda: start_if(1, copies[0] + copies[1]), out_it)

time: 27.8 us -> 27.7 us (level)
  no operation moved by 1% of the time
where the time goes in v6:
time: 27.7 us; the launch traced here: 27.5 us
  Pallas kernels  26.9 us (97%)
  between operations  0.64 us (2%)
    pallas_call x1, Pallas kernels, per_device(): pl.pallas_call(functools.partial(kernel, counts), out_shape=(pltpu.VMEM(f...  26 us
    pallas_call x1, Pallas kernels, per_device(): pl.pallas_call(hand_over, out_shape=(jax.ShapeDtypeStruct(field, F32),) *...  0.89 us

profile of v6, /device:TPU:0, one launch (start us, length us, event | category | flops | bytes accessed | tf_op | source)
XLA Modules:
  0.0 27.5 jit_solution(11422166870067145701)
XLA Ops:
  0.6 26.0 %shard_map.95 = (f32[768,128]{1,0:T(8,128)S(1)}, f32[768,128]{1,0:T(8,128)S(1)}) custom-call(s32[4]{0:T(128)} %bc_hbm.1, s32[2]{0:T(128)} %bitcast.19, f32[768,128]{1,0:T(8,128)} %bitcast.17, f32[768,128]{1,0:T(8,128)} %bitcast.18, f32[2304,128]{1,0:T(8,128)} %bitcast.16, f32[4608,128]{1,0:T(8,128)} %bitcast.15, bf16[2,2,24,12,16,128]{5,4,3,2,1,0:T(8,128)(2,1)} %bitcast.13, ...), custom_call_target="tpu_custom_call" | custom-call | tf_op jit(solution)/shard_map/pallas_call | solution.py:675
  26.6 0.9 %shard_map.96 = (f32[768,128]{1,0:T(8,128)}, f32[768,128]{1,0:T(8,128)}) custom-call(f32[768,128]{1,0:T(8,128)S(1)} %get-tuple-element.6.it_in, f32[768,128]{1,0:T(8,128)S(1)} %get-tuple-element.7.res_in), custom_call_target="tpu_custom_call" | custom-call | tf_op jit(solution)/shard_map/pallas_call | solution.py:734
